TPU v7x, 16 devices: a 4x2x1 block of a 4x4x8 slice. The times are simulated.
16 devices in a mesh: rep: 2 (over y, z), stage: 8 (over x, core).
Axes of the slice: x: 4, y: 2, z: 1, core: 2. Of those that a mesh axis runs over, the one named last changes fastest.
The devices are a block of a 4x4x8 slice.
Arguments:
- embeds: bfloat16 [16, 2, 256, 1024], P('rep'), parts along dimension 0
- targets: bfloat16 [16, 2, 256, 1024], P('rep'), parts along dimension 0
- w_qkv: bfloat16 [8, 1024, 3072], P('stage')
- w_out: bfloat16 [8, 16, 64, 1024], P('stage')
- w_up: bfloat16 [8, 1024, 4096], P('stage')
- w_down: bfloat16 [8, 4096, 1024], P('stage')
Outputs:
- output 1: float32 [2], P('rep'), parts along dimension 0
- output 2: float32 [16, 1024, 3072], P(('rep', 'stage')), parts along dimension 0
- output 3: float32 [16, 16, 64, 1024], P(('rep', 'stage')), parts along dimension 0
- output 4: float32 [16, 1024, 4096], P(('rep', 'stage')), parts along dimension 0
- output 5: float32 [16, 4096, 1024], P(('rep', 'stage')), parts along dimension 0
- output 6: bfloat16 [16, 2, 256, 1024], P('rep'), parts along dimension 0
There are 2 independent parts. A program takes and returns all parts, laid end to end along the dimension named above; an argument that names none is the same for every part.
All inputs are finite; a program needn't handle non-finite values.
Results may differ from a plain program's by a relative error of at most 0.02.
Values are sent between devices in bfloat16 or wider.
A program may use at most 768 MiB of HBM per device.

v0:
```python
import jax
import jax.numpy as jnp
from jax import lax
from jax.sharding import PartitionSpec as P

NORM_EPS = 1e-6
NEG_BIG = -1e30


def rms_norm(vals):
    return vals * lax.rsqrt(jnp.mean(vals * vals, axis=-1, keepdims=True) + NORM_EPS)


def norm_bf16(vals):
    return rms_norm(vals).astype(jnp.bfloat16)


def gelu_bf16(pre_act):
    return jax.nn.gelu(pre_act.astype(jnp.float32)).astype(jnp.bfloat16)


def probs_bf16(scores):
    seq_len = scores.shape[-1]
    causal = jnp.arange(seq_len)[:, None] >= jnp.arange(seq_len)[None, :]
    return jax.nn.softmax(jnp.where(causal, scores.astype(jnp.float32), NEG_BIG), axis=-1).astype(jnp.bfloat16)


def layer_forward(act_in, w_qkv, w_out, w_up, w_down):
    batch_size, seq_len = act_in.shape[0], act_in.shape[1]
    num_heads, head_dim = w_out.shape[0], w_out.shape[1]
    act_f = act_in.astype(jnp.float32)
    normed = norm_bf16(act_f)
    qkv_flat = jnp.einsum('bsd,de->bse', normed, w_qkv, preferred_element_type=jnp.float32).astype(jnp.bfloat16)
    qkv_heads = qkv_flat.reshape(batch_size, seq_len, 3, num_heads, head_dim)
    scores = (jnp.einsum('bqhd,bkhd->bhqk', qkv_heads[:, :, 0], qkv_heads[:, :, 1], preferred_element_type=jnp.float32) * head_dim ** -0.5).astype(jnp.bfloat16)
    attn_probs = probs_bf16(scores)
    context = jnp.einsum('bhqk,bkhd->bqhd', attn_probs, qkv_heads[:, :, 2], preferred_element_type=jnp.float32).astype(jnp.bfloat16)
    hidden = act_f + jnp.einsum('bqhd,hde->bqe', context, w_out, preferred_element_type=jnp.float32)
    hidden_f = hidden.astype(jnp.bfloat16).astype(jnp.float32)
    normed2 = norm_bf16(hidden_f)
    pre_act = jnp.einsum('bsd,df->bsf', normed2, w_up, preferred_element_type=jnp.float32).astype(jnp.bfloat16)
    gelu_out = gelu_bf16(pre_act)
    act_out = (hidden_f + jnp.einsum('bsf,fd->bsd', gelu_out, w_down, preferred_element_type=jnp.float32)).astype(jnp.bfloat16)
    saved_vals = (act_f, normed, qkv_heads, scores, attn_probs, context, hidden_f, normed2, pre_act, gelu_out)
    return act_out, saved_vals


def layer_backward(grad_out, saved_vals, w_qkv, w_out, w_up, w_down):
    act_f, normed, qkv_heads, scores, attn_probs, context, hidden_f, normed2, pre_act, gelu_out = saved_vals
    batch_size, seq_len = grad_out.shape[0], grad_out.shape[1]
    head_dim = qkv_heads.shape[-1]
    d_wdown = jnp.einsum('bsf,bsd->fd', gelu_out, grad_out, preferred_element_type=jnp.float32)
    d_gelu = jnp.einsum('bsd,fd->bsf', grad_out, w_down, preferred_element_type=jnp.float32).astype(jnp.bfloat16)
    d_pre = jax.vjp(gelu_bf16, pre_act)[1](d_gelu)[0]
    d_wup = jnp.einsum('bsd,bsf->df', normed2, d_pre, preferred_element_type=jnp.float32)
    d_norm2 = jnp.einsum('bsf,df->bsd', d_pre, w_up, preferred_element_type=jnp.float32).astype(jnp.bfloat16)
    d_hidden = (grad_out.astype(jnp.float32) + jax.vjp(norm_bf16, hidden_f)[1](d_norm2)[0]).astype(jnp.bfloat16)
    d_wout = jnp.einsum('bqhd,bqe->hde', context, d_hidden, preferred_element_type=jnp.float32)
    d_context = jnp.einsum('bqe,hde->bqhd', d_hidden, w_out, preferred_element_type=jnp.float32).astype(jnp.bfloat16)
    d_probs = jnp.einsum('bqhd,bkhd->bhqk', d_context, qkv_heads[:, :, 2], preferred_element_type=jnp.float32).astype(jnp.bfloat16)
    d_value = jnp.einsum('bhqk,bqhd->bkhd', attn_probs, d_context, preferred_element_type=jnp.float32).astype(jnp.bfloat16)
    d_scores = jax.vjp(probs_bf16, scores)[1](d_probs)[0]
    d_query = (jnp.einsum('bhqk,bkhd->bqhd', d_scores, qkv_heads[:, :, 1], preferred_element_type=jnp.float32) * head_dim ** -0.5).astype(jnp.bfloat16)
    d_key = (jnp.einsum('bhqk,bqhd->bkhd', d_scores, qkv_heads[:, :, 0], preferred_element_type=jnp.float32) * head_dim ** -0.5).astype(jnp.bfloat16)
    d_qkv = jnp.stack([d_query, d_key, d_value], axis=2).reshape(batch_size, seq_len, -1)
    d_wqkv = jnp.einsum('bsd,bse->de', normed, d_qkv, preferred_element_type=jnp.float32)
    d_norm1 = jnp.einsum('bse,de->bsd', d_qkv, w_qkv, preferred_element_type=jnp.float32).astype(jnp.bfloat16)
    d_act = (d_hidden.astype(jnp.float32) + jax.vjp(norm_bf16, act_f)[1](d_norm1)[0]).astype(jnp.bfloat16)
    return d_act, (d_wqkv, d_wout, d_wup, d_wdown)


def solution(mesh):
    num_stages = mesh.shape['stage']
    fwd_perm = [(src_stage, src_stage + 1) for src_stage in range(num_stages - 1)]
    bwd_perm = [(src_stage + 1, src_stage) for src_stage in range(num_stages - 1)]

    def stage_program(embeds, targets, w_qkv, w_out, w_up, w_down):
        weights = (w_qkv[0], w_out[0], w_up[0], w_down[0])
        stage_idx = lax.axis_index('stage')
        is_first = stage_idx == 0
        is_last = stage_idx == num_stages - 1
        num_micro, batch_size, seq_len, model_dim = embeds.shape
        norm_count = num_micro * batch_size * seq_len * model_dim
        zero_act = jnp.zeros((batch_size, seq_len, model_dim), jnp.bfloat16)

        def run_forward(layer_in):
            return layer_forward(layer_in, *weights)[0]

        def skip_forward(layer_in):
            return zero_act

        def run_backward(bwd_in, grad_in, grad_acc):
            saved_vals = layer_forward(bwd_in, *weights)[1]
            d_act, d_weights = layer_backward(grad_in, saved_vals, *weights)
            return d_act, tuple(acc_w + grad_w for acc_w, grad_w in zip(grad_acc, d_weights))

        def skip_backward(bwd_in, grad_in, grad_acc):
            return zero_act, grad_acc

        def run_tick(tick_idx, loop_state):
            recv_act, recv_grad, saved_inputs, dx_buf, grad_acc, loss_acc = loop_state
            fwd_micro = tick_idx - stage_idx
            fwd_ok = (fwd_micro >= 0) & (fwd_micro < num_micro)
            fwd_slot = jnp.clip(fwd_micro, 0, num_micro - 1)
            bwd_micro = tick_idx - 2 * (num_stages - 1) + stage_idx
            bwd_ok = (bwd_micro >= 0) & (bwd_micro < num_micro)
            bwd_slot = jnp.clip(bwd_micro, 0, num_micro - 1)
            embed_m = lax.dynamic_index_in_dim(embeds, fwd_slot, 0, keepdims=False)
            layer_in = jnp.where(is_first, embed_m, recv_act)
            act_out = lax.cond(fwd_ok, run_forward, skip_forward, layer_in)
            old_input = lax.dynamic_index_in_dim(saved_inputs, fwd_slot, 0, keepdims=False)
            saved_inputs = lax.dynamic_update_index_in_dim(saved_inputs, jnp.where(fwd_ok, layer_in, old_input), fwd_slot, 0)
            target_m = lax.dynamic_index_in_dim(targets, bwd_slot, 0, keepdims=False)
            err_vals = act_out.astype(jnp.float32) - target_m.astype(jnp.float32)
            seed_grad = (err_vals / norm_count).astype(jnp.bfloat16)
            loss_acc = loss_acc + jnp.where(is_last & bwd_ok, 0.5 * jnp.sum(err_vals * err_vals) / norm_count, 0.0)
            grad_in = jnp.where(is_last, seed_grad, recv_grad)
            bwd_in = lax.dynamic_index_in_dim(saved_inputs, bwd_slot, 0, keepdims=False)
            d_act, grad_acc = lax.cond(bwd_ok, run_backward, skip_backward, bwd_in, grad_in, grad_acc)
            old_dx = lax.dynamic_index_in_dim(dx_buf, bwd_slot, 0, keepdims=False)
            dx_buf = lax.dynamic_update_index_in_dim(dx_buf, jnp.where(is_first & bwd_ok, d_act, old_dx), bwd_slot, 0)
            recv_act = lax.ppermute(act_out, 'stage', fwd_perm)
            recv_grad = lax.ppermute(d_act, 'stage', bwd_perm)
            return recv_act, recv_grad, saved_inputs, dx_buf, grad_acc, loss_acc

        zero_grads = tuple(jnp.zeros(w_one.shape, jnp.float32) for w_one in weights)
        loop_state = (zero_act, zero_act, jnp.zeros_like(embeds), jnp.zeros_like(embeds), zero_grads, jnp.zeros((), jnp.float32))
        loop_state = lax.fori_loop(0, num_micro + 2 * num_stages - 2, run_tick, loop_state)
        dx_buf, grad_acc, loss_acc = loop_state[3], loop_state[4], loop_state[5]
        d_embeds = lax.psum(dx_buf, 'stage')
        total_loss = lax.psum(loss_acc, 'stage').reshape(1)
        return (total_loss,) + tuple(g_one[None] for g_one in grad_acc) + (d_embeds,)

    act_spec = P('rep', None, None, None)
    w3_spec = P('stage', None, None)
    g3_spec = P(('rep', 'stage'), None, None)
    in_specs = (act_spec, act_spec, w3_spec, P('stage', None, None, None), w3_spec, w3_spec)
    out_specs = (P('rep'), g3_spec, P(('rep', 'stage'), None, None, None), g3_spec, g3_spec, act_spec)
    return jax.shard_map(stage_program, mesh=mesh, in_specs=in_specs, out_specs=out_specs, check_vma=False)
```

profile of v0, /device:TPU:112, one launch (start us, length us, event | category | flops | bytes accessed | tf_op | source)
XLA Modules:
  0.0 3318.3 jit_solution(9812785829030488221)
XLA Ops:
  43.7 3163.0 %while.31 = (s32[]{:T(128)}, bf16[2,256,1024]{2,1,0:T(8,128)(2,1)}, bf16[2,256,1024]{2,1,0:T(8,128)(2,1)}, bf16[8,2,256,1024]{3,2,1,0:T(8,128)(2,1)}, bf16[8,2,2...) while((s32[]{:T(128)}, bf16[2,256,1024]{2,1,0:T(8,128)(2,1)}, ...), condition=%wide.region_17.18_spmd, body=%wide.region_0.17_spmd.sunk | while | flops 49615626240 | bytes 658242880 | solution.py:128
  48.4 42.8 %conditional.4 = (bf16[2,256,1024]{2,1,0:T(8,128)(2,1)}, f32[2,256,1024]{2,1,0:T(8,128)}) conditional(s32[]{:T(128)} %convert_element_type.516, () %tuple.80, (bf16[2,256,1024]{2,1,0:T(8,128)(2,1)S(1)}, bf16[1024,3072]{1,0:T(8,128)(2,1)S(1)}, bf16[16,64,1024]{2,1,0:T(8,128)(2,1)}, bf16[1024,4096]{1,0:T(8,128)(2,1)}, ...), branch_computations={%region_1.1_spmd, %region_2.6_spmd} | conditional | flops 13477938176 | bytes 89342024 | solution.py:110
  111.4 42.2 %conditional.4 = (bf16[2,256,1024]{2,1,0:T(8,128)(2,1)}, f32[2,256,1024]{2,1,0:T(8,128)}) conditional(s32[]{:T(128)} %convert_element_type.516, () %tuple.80, (bf16[2,256,1024]{2,1,0:T(8,128)(2,1)S(1)}, bf16[1024,3072]{1,0:T(8,128)(2,1)S(1)}, bf16[16,64,1024]{2,1,0:T(8,128)(2,1)}, bf16[1024,4096]{1,0:T(8,128)(2,1)}, ...), branch_computations={%region_1.1_spmd, %region_2.6_spmd} | conditional | flops 13477938176 | bytes 89342024 | solution.py:110
  172.4 41.7 %conditional.4 = (bf16[2,256,1024]{2,1,0:T(8,128)(2,1)}, f32[2,256,1024]{2,1,0:T(8,128)}) conditional(s32[]{:T(128)} %convert_element_type.516, () %tuple.80, (bf16[2,256,1024]{2,1,0:T(8,128)(2,1)S(1)}, bf16[1024,3072]{1,0:T(8,128)(2,1)S(1)}, bf16[16,64,1024]{2,1,0:T(8,128)(2,1)}, bf16[1024,4096]{1,0:T(8,128)(2,1)}, ...), branch_computations={%region_1.1_spmd, %region_2.6_spmd} | conditional | flops 13477938176 | bytes 89342024 | solution.py:110
  242.4 41.7 %conditional.4 = (bf16[2,256,1024]{2,1,0:T(8,128)(2,1)}, f32[2,256,1024]{2,1,0:T(8,128)}) conditional(s32[]{:T(128)} %convert_element_type.516, () %tuple.80, (bf16[2,256,1024]{2,1,0:T(8,128)(2,1)S(1)}, bf16[1024,3072]{1,0:T(8,128)(2,1)S(1)}, bf16[16,64,1024]{2,1,0:T(8,128)(2,1)}, bf16[1024,4096]{1,0:T(8,128)(2,1)}, ...), branch_computations={%region_1.1_spmd, %region_2.6_spmd} | conditional | flops 13477938176 | bytes 89342024 | solution.py:110
  313.0 41.7 %conditional.4 = (bf16[2,256,1024]{2,1,0:T(8,128)(2,1)}, f32[2,256,1024]{2,1,0:T(8,128)}) conditional(s32[]{:T(128)} %convert_element_type.516, () %tuple.80, (bf16[2,256,1024]{2,1,0:T(8,128)(2,1)S(1)}, bf16[1024,3072]{1,0:T(8,128)(2,1)S(1)}, bf16[16,64,1024]{2,1,0:T(8,128)(2,1)}, bf16[1024,4096]{1,0:T(8,128)(2,1)}, ...), branch_computations={%region_1.1_spmd, %region_2.6_spmd} | conditional | flops 13477938176 | bytes 89342024 | solution.py:110
  595.8 52.7 %collective-permute-start = (bf16[2,256,1024]{2,1,0:T(8,128)(2,1)}, bf16[2,256,1024]{2,1,0:T(8,128)(2,1)}, u32[]{:S(2)}, u32[]{:S(2)}) collective-permute-start(bf16[2,256,1024]{2,1,0:T(8,128)(2,1)} %get-tuple-element.778), channel_id=1, source_target_pairs={{0,1},{1,2},{2,3},{3,4},{4,5},{5,6},{6,7},{8,9},{9,10},{10,11},{11... | collective-permute-start | bytes 3145736 | tf_op jit(solution)/shard_map/while/body/eval_jaxpr/ppermute | solution.py:122
  758.3 57.6 %collective-permute-done.1 = bf16[2,256,1024]{2,1,0:T(8,128)(2,1)S(1)} collective-permute-done((bf16[2,256,1024]{2,1,0:T(8,128)(2,1)}, bf16[2,256,1024]{2,1,0:T(8,128)(2,1)S(1)}, u32[]{:S(2)}, u32[]{:S(2)}) %collective-permute-start.1) | collective-permute-done | bytes 1048608 | tf_op jit(solution)/shard_map/while/body/eval_jaxpr/ppermute | solution.py:123
  824.2 204.4 %collective-permute-start = (bf16[2,256,1024]{2,1,0:T(8,128)(2,1)}, bf16[2,256,1024]{2,1,0:T(8,128)(2,1)}, u32[]{:S(2)}, u32[]{:S(2)}) collective-permute-start(bf16[2,256,1024]{2,1,0:T(8,128)(2,1)} %get-tuple-element.778), channel_id=1, source_target_pairs={{0,1},{1,2},{2,3},{3,4},{4,5},{5,6},{6,7},{8,9},{9,10},{10,11},{11... | collective-permute-start | bytes 3145736 | tf_op jit(solution)/shard_map/while/body/eval_jaxpr/ppermute | solution.py:122
  1037.6 107.5 %collective-permute-done.1 = bf16[2,256,1024]{2,1,0:T(8,128)(2,1)S(1)} collective-permute-done((bf16[2,256,1024]{2,1,0:T(8,128)(2,1)}, bf16[2,256,1024]{2,1,0:T(8,128)(2,1)S(1)}, u32[]{:S(2)}, u32[]{:S(2)}) %collective-permute-start.1) | collective-permute-done | bytes 1048608 | tf_op jit(solution)/shard_map/while/body/eval_jaxpr/ppermute | solution.py:123
  1153.5 165.9 %collective-permute-start = (bf16[2,256,1024]{2,1,0:T(8,128)(2,1)}, bf16[2,256,1024]{2,1,0:T(8,128)(2,1)}, u32[]{:S(2)}, u32[]{:S(2)}) collective-permute-start(bf16[2,256,1024]{2,1,0:T(8,128)(2,1)} %get-tuple-element.778), channel_id=1, source_target_pairs={{0,1},{1,2},{2,3},{3,4},{4,5},{5,6},{6,7},{8,9},{9,10},{10,11},{11... | collective-permute-start | bytes 3145736 | tf_op jit(solution)/shard_map/while/body/eval_jaxpr/ppermute | solution.py:122
  1328.3 156.8 %collective-permute-done.1 = bf16[2,256,1024]{2,1,0:T(8,128)(2,1)S(1)} collective-permute-done((bf16[2,256,1024]{2,1,0:T(8,128)(2,1)}, bf16[2,256,1024]{2,1,0:T(8,128)(2,1)S(1)}, u32[]{:S(2)}, u32[]{:S(2)}) %collective-permute-start.1) | collective-permute-done | bytes 1048608 | tf_op jit(solution)/shard_map/while/body/eval_jaxpr/ppermute | solution.py:123
  1493.5 158.8 %collective-permute-start = (bf16[2,256,1024]{2,1,0:T(8,128)(2,1)}, bf16[2,256,1024]{2,1,0:T(8,128)(2,1)}, u32[]{:S(2)}, u32[]{:S(2)}) collective-permute-start(bf16[2,256,1024]{2,1,0:T(8,128)(2,1)} %get-tuple-element.778), channel_id=1, source_target_pairs={{0,1},{1,2},{2,3},{3,4},{4,5},{5,6},{6,7},{8,9},{9,10},{10,11},{11... | collective-permute-start | bytes 3145736 | tf_op jit(solution)/shard_map/while/body/eval_jaxpr/ppermute | solution.py:122
  1661.2 130.9 %collective-permute-done.1 = bf16[2,256,1024]{2,1,0:T(8,128)(2,1)S(1)} collective-permute-done((bf16[2,256,1024]{2,1,0:T(8,128)(2,1)}, bf16[2,256,1024]{2,1,0:T(8,128)(2,1)S(1)}, u32[]{:S(2)}, u32[]{:S(2)}) %collective-permute-start.1) | collective-permute-done | bytes 1048608 | tf_op jit(solution)/shard_map/while/body/eval_jaxpr/ppermute | solution.py:123
  1800.5 55.9 %collective-permute-start = (bf16[2,256,1024]{2,1,0:T(8,128)(2,1)}, bf16[2,256,1024]{2,1,0:T(8,128)(2,1)}, u32[]{:S(2)}, u32[]{:S(2)}) collective-permute-start(bf16[2,256,1024]{2,1,0:T(8,128)(2,1)} %get-tuple-element.778), channel_id=1, source_target_pairs={{0,1},{1,2},{2,3},{3,4},{4,5},{5,6},{6,7},{8,9},{9,10},{10,11},{11... | collective-permute-start | bytes 3145736 | tf_op jit(solution)/shard_map/while/body/eval_jaxpr/ppermute | solution.py:122
  1859.5 130.0 %conditional.5 = (bf16[2,256,1024]{2,1,0:T(8,128)(2,1)}, f32[1024,3072]{1,0:T(8,128)}, f32[16,64,1024]{2,1,0:T(8,128)}, f32[1024,4096]{1,0:T(8,128)}, f32[4096,1024]{1,0:T(8,128)}) conditional(s32[]{:T(128)} %convert_element_type.517, (f32[1024,3072]{1,0:T(8,128)}, f32[16,64,1024]{2,1,0:T(8,128)}, f32[1024,4096]{1,0:T(8,128)}, ...), branch_computations={%region_7.7_spmd, %region_8.15_spmd} | conditional | flops 36132970496 | bytes 514373216 | solution.py:119
  2023.4 130.1 %conditional.5 = (bf16[2,256,1024]{2,1,0:T(8,128)(2,1)}, f32[1024,3072]{1,0:T(8,128)}, f32[16,64,1024]{2,1,0:T(8,128)}, f32[1024,4096]{1,0:T(8,128)}, f32[4096,1024]{1,0:T(8,128)}) conditional(s32[]{:T(128)} %convert_element_type.517, (f32[1024,3072]{1,0:T(8,128)}, f32[16,64,1024]{2,1,0:T(8,128)}, f32[1024,4096]{1,0:T(8,128)}, ...), branch_computations={%region_7.7_spmd, %region_8.15_spmd} | conditional | flops 36132970496 | bytes 514373216 | solution.py:119
  2223.7 130.1 %conditional.5 = (bf16[2,256,1024]{2,1,0:T(8,128)(2,1)}, f32[1024,3072]{1,0:T(8,128)}, f32[16,64,1024]{2,1,0:T(8,128)}, f32[1024,4096]{1,0:T(8,128)}, f32[4096,1024]{1,0:T(8,128)}) conditional(s32[]{:T(128)} %convert_element_type.517, (f32[1024,3072]{1,0:T(8,128)}, f32[16,64,1024]{2,1,0:T(8,128)}, f32[1024,4096]{1,0:T(8,128)}, ...), branch_computations={%region_7.7_spmd, %region_8.15_spmd} | conditional | flops 36132970496 | bytes 514373216 | solution.py:119
  2412.2 130.1 %conditional.5 = (bf16[2,256,1024]{2,1,0:T(8,128)(2,1)}, f32[1024,3072]{1,0:T(8,128)}, f32[16,64,1024]{2,1,0:T(8,128)}, f32[1024,4096]{1,0:T(8,128)}, f32[4096,1024]{1,0:T(8,128)}) conditional(s32[]{:T(128)} %convert_element_type.517, (f32[1024,3072]{1,0:T(8,128)}, f32[16,64,1024]{2,1,0:T(8,128)}, f32[1024,4096]{1,0:T(8,128)}, ...), branch_computations={%region_7.7_spmd, %region_8.15_spmd} | conditional | flops 36132970496 | bytes 514373216 | solution.py:119
  2576.1 130.1 %conditional.5 = (bf16[2,256,1024]{2,1,0:T(8,128)(2,1)}, f32[1024,3072]{1,0:T(8,128)}, f32[16,64,1024]{2,1,0:T(8,128)}, f32[1024,4096]{1,0:T(8,128)}, f32[4096,1024]{1,0:T(8,128)}) conditional(s32[]{:T(128)} %convert_element_type.517, (f32[1024,3072]{1,0:T(8,128)}, f32[16,64,1024]{2,1,0:T(8,128)}, f32[1024,4096]{1,0:T(8,128)}, ...), branch_computations={%region_7.7_spmd, %region_8.15_spmd} | conditional | flops 36132970496 | bytes 514373216 | solution.py:119
  2740.0 130.1 %conditional.5 = (bf16[2,256,1024]{2,1,0:T(8,128)(2,1)}, f32[1024,3072]{1,0:T(8,128)}, f32[16,64,1024]{2,1,0:T(8,128)}, f32[1024,4096]{1,0:T(8,128)}, f32[4096,1024]{1,0:T(8,128)}) conditional(s32[]{:T(128)} %convert_element_type.517, (f32[1024,3072]{1,0:T(8,128)}, f32[16,64,1024]{2,1,0:T(8,128)}, f32[1024,4096]{1,0:T(8,128)}, ...), branch_computations={%region_7.7_spmd, %region_8.15_spmd} | conditional | flops 36132970496 | bytes 514373216 | solution.py:119
  2903.8 130.1 %conditional.5 = (bf16[2,256,1024]{2,1,0:T(8,128)(2,1)}, f32[1024,3072]{1,0:T(8,128)}, f32[16,64,1024]{2,1,0:T(8,128)}, f32[1024,4096]{1,0:T(8,128)}, f32[4096,1024]{1,0:T(8,128)}) conditional(s32[]{:T(128)} %convert_element_type.517, (f32[1024,3072]{1,0:T(8,128)}, f32[16,64,1024]{2,1,0:T(8,128)}, f32[1024,4096]{1,0:T(8,128)}, ...), branch_computations={%region_7.7_spmd, %region_8.15_spmd} | conditional | flops 36132970496 | bytes 514373216 | solution.py:119
  3067.7 130.1 %conditional.5 = (bf16[2,256,1024]{2,1,0:T(8,128)(2,1)}, f32[1024,3072]{1,0:T(8,128)}, f32[16,64,1024]{2,1,0:T(8,128)}, f32[1024,4096]{1,0:T(8,128)}, f32[4096,1024]{1,0:T(8,128)}) conditional(s32[]{:T(128)} %convert_element_type.517, (f32[1024,3072]{1,0:T(8,128)}, f32[16,64,1024]{2,1,0:T(8,128)}, f32[1024,4096]{1,0:T(8,128)}, ...), branch_computations={%region_7.7_spmd, %region_8.15_spmd} | conditional | flops 36132970496 | bytes 514373216 | solution.py:119
  3220.6 82.4 %all-reduce.2.cloned.1.call-done = bf16[8,2,256,1024]{3,2,1,0:T(8,128)(2,1)} async-done(((bf16[8,2,256,1024]{3,2,1,0:T(8,128)(2,1)}), bf16[8,2,256,1024]{3,2,1,0:T(8,128)(2,1)}) %all-reduce.2.cloned.1.call-update) | async-done | bytes 8388624 | tf_op jit(solution)/shard_map/psum | solution.py:130
  (1058 shorter events, 2285.1 us)
Async XLA Ops:
  7.2 3295.8 %all-reduce.2.cloned.1.call-start = ((), (), s32[]{:S(2)}) async-start(), calls=%async_computation | async-start | bytes 16777216 | tf_op jit(solution)/shard_map/psum | solution.py:130
  214.1 22.7 collective-permute-start
  284.1 23.2 collective-permute-start
  354.7 22.7 collective-permute-start
  424.7 22.7 collective-permute-start
  595.8 61.6 %collective-permute-start = (bf16[2,256,1024]{2,1,0:T(8,128)(2,1)}, bf16[2,256,1024]{2,1,0:T(8,128)(2,1)}, u32[]{:S(2)}, u32[]{:S(2)}) collective-permute-start(bf16[2,256,1024]{2,1,0:T(8,128)(2,1)} %get-tuple-element.778), channel_id=1, source_target_pairs={{0,1},{1,2},{2,3},{3,4},{4,5},{5,6},{6,7},{8,9},{9,10},{10,11},{11... | collective-permute-start | bytes 3145736 | tf_op jit(solution)/shard_map/while/body/eval_jaxpr/ppermute | solution.py:122
  665.8 22.7 collective-permute-start
  683.8 41.9 %collective-permute-start.1 = (bf16[2,256,1024]{2,1,0:T(8,128)(2,1)}, bf16[2,256,1024]{2,1,0:T(8,128)(2,1)S(1)}, u32[]{:S(2)}, u32[]{:S(2)}) collective-permute-start(bf16[2,256,1024]{2,1,0:T(8,128)(2,1)} %get-tuple-element.782), channel_id=1, source_target_pairs={{1,0},{2,1},{3,2},{4,3},{5,4},{6,5},{7,6},{9,8},{10,9},{11,10},{12... | collective-permute-start | bytes 3145736 | tf_op jit(solution)/shard_map/while/body/eval_jaxpr/ppermute | solution.py:123
  734.0 24.3 collective-permute-start
  753.6 62.3 %collective-permute-start.1 = (bf16[2,256,1024]{2,1,0:T(8,128)(2,1)}, bf16[2,256,1024]{2,1,0:T(8,128)(2,1)S(1)}, u32[]{:S(2)}, u32[]{:S(2)}) collective-permute-start(bf16[2,256,1024]{2,1,0:T(8,128)(2,1)} %get-tuple-element.782), channel_id=1, source_target_pairs={{1,0},{2,1},{3,2},{4,3},{5,4},{6,5},{7,6},{9,8},{10,9},{11,10},{12... | collective-permute-start | bytes 3145736 | tf_op jit(solution)/shard_map/while/body/eval_jaxpr/ppermute | solution.py:123
  824.2 213.4 %collective-permute-start = (bf16[2,256,1024]{2,1,0:T(8,128)(2,1)}, bf16[2,256,1024]{2,1,0:T(8,128)(2,1)}, u32[]{:S(2)}, u32[]{:S(2)}) collective-permute-start(bf16[2,256,1024]{2,1,0:T(8,128)(2,1)} %get-tuple-element.778), channel_id=1, source_target_pairs={{0,1},{1,2},{2,3},{3,4},{4,5},{5,6},{6,7},{8,9},{9,10},{10,11},{11... | collective-permute-start | bytes 3145736 | tf_op jit(solution)/shard_map/while/body/eval_jaxpr/ppermute | solution.py:122
  1032.9 112.2 %collective-permute-start.1 = (bf16[2,256,1024]{2,1,0:T(8,128)(2,1)}, bf16[2,256,1024]{2,1,0:T(8,128)(2,1)S(1)}, u32[]{:S(2)}, u32[]{:S(2)}) collective-permute-start(bf16[2,256,1024]{2,1,0:T(8,128)(2,1)} %get-tuple-element.782), channel_id=1, source_target_pairs={{1,0},{2,1},{3,2},{4,3},{5,4},{6,5},{7,6},{9,8},{10,9},{11,10},{12... | collective-permute-start | bytes 3145736 | tf_op jit(solution)/shard_map/while/body/eval_jaxpr/ppermute | solution.py:123
  1153.5 174.8 %collective-permute-start = (bf16[2,256,1024]{2,1,0:T(8,128)(2,1)}, bf16[2,256,1024]{2,1,0:T(8,128)(2,1)}, u32[]{:S(2)}, u32[]{:S(2)}) collective-permute-start(bf16[2,256,1024]{2,1,0:T(8,128)(2,1)} %get-tuple-element.778), channel_id=1, source_target_pairs={{0,1},{1,2},{2,3},{3,4},{4,5},{5,6},{6,7},{8,9},{9,10},{10,11},{11... | collective-permute-start | bytes 3145736 | tf_op jit(solution)/shard_map/while/body/eval_jaxpr/ppermute | solution.py:122
  1323.6 161.5 %collective-permute-start.1 = (bf16[2,256,1024]{2,1,0:T(8,128)(2,1)}, bf16[2,256,1024]{2,1,0:T(8,128)(2,1)S(1)}, u32[]{:S(2)}, u32[]{:S(2)}) collective-permute-start(bf16[2,256,1024]{2,1,0:T(8,128)(2,1)} %get-tuple-element.782), channel_id=1, source_target_pairs={{1,0},{2,1},{3,2},{4,3},{5,4},{6,5},{7,6},{9,8},{10,9},{11,10},{12... | collective-permute-start | bytes 3145736 | tf_op jit(solution)/shard_map/while/body/eval_jaxpr/ppermute | solution.py:123
  1493.5 167.8 %collective-permute-start = (bf16[2,256,1024]{2,1,0:T(8,128)(2,1)}, bf16[2,256,1024]{2,1,0:T(8,128)(2,1)}, u32[]{:S(2)}, u32[]{:S(2)}) collective-permute-start(bf16[2,256,1024]{2,1,0:T(8,128)(2,1)} %get-tuple-element.778), channel_id=1, source_target_pairs={{0,1},{1,2},{2,3},{3,4},{4,5},{5,6},{6,7},{8,9},{9,10},{10,11},{11... | collective-permute-start | bytes 3145736 | tf_op jit(solution)/shard_map/while/body/eval_jaxpr/ppermute | solution.py:122
  1656.5 135.6 %collective-permute-start.1 = (bf16[2,256,1024]{2,1,0:T(8,128)(2,1)}, bf16[2,256,1024]{2,1,0:T(8,128)(2,1)S(1)}, u32[]{:S(2)}, u32[]{:S(2)}) collective-permute-start(bf16[2,256,1024]{2,1,0:T(8,128)(2,1)} %get-tuple-element.782), channel_id=1, source_target_pairs={{1,0},{2,1},{3,2},{4,3},{5,4},{6,5},{7,6},{9,8},{10,9},{11,10},{12... | collective-permute-start | bytes 3145736 | tf_op jit(solution)/shard_map/while/body/eval_jaxpr/ppermute | solution.py:123
  1800.5 194.9 %collective-permute-start = (bf16[2,256,1024]{2,1,0:T(8,128)(2,1)}, bf16[2,256,1024]{2,1,0:T(8,128)(2,1)}, u32[]{:S(2)}, u32[]{:S(2)}) collective-permute-start(bf16[2,256,1024]{2,1,0:T(8,128)(2,1)} %get-tuple-element.778), channel_id=1, source_target_pairs={{0,1},{1,2},{2,3},{3,4},{4,5},{5,6},{6,7},{8,9},{9,10},{10,11},{11... | collective-permute-start | bytes 3145736 | tf_op jit(solution)/shard_map/while/body/eval_jaxpr/ppermute | solution.py:122
  2007.6 151.9 %collective-permute-start = (bf16[2,256,1024]{2,1,0:T(8,128)(2,1)}, bf16[2,256,1024]{2,1,0:T(8,128)(2,1)}, u32[]{:S(2)}, u32[]{:S(2)}) collective-permute-start(bf16[2,256,1024]{2,1,0:T(8,128)(2,1)} %get-tuple-element.778), channel_id=1, source_target_pairs={{0,1},{1,2},{2,3},{3,4},{4,5},{5,6},{6,7},{8,9},{9,10},{10,11},{11... | collective-permute-start | bytes 3145736 | tf_op jit(solution)/shard_map/while/body/eval_jaxpr/ppermute | solution.py:122
  2184.2 175.6 %collective-permute-start = (bf16[2,256,1024]{2,1,0:T(8,128)(2,1)}, bf16[2,256,1024]{2,1,0:T(8,128)(2,1)}, u32[]{:S(2)}, u32[]{:S(2)}) collective-permute-start(bf16[2,256,1024]{2,1,0:T(8,128)(2,1)} %get-tuple-element.778), channel_id=1, source_target_pairs={{0,1},{1,2},{2,3},{3,4},{4,5},{5,6},{6,7},{8,9},{9,10},{10,11},{11... | collective-permute-start | bytes 3145736 | tf_op jit(solution)/shard_map/while/body/eval_jaxpr/ppermute | solution.py:122
  2372.0 176.3 %collective-permute-start = (bf16[2,256,1024]{2,1,0:T(8,128)(2,1)}, bf16[2,256,1024]{2,1,0:T(8,128)(2,1)}, u32[]{:S(2)}, u32[]{:S(2)}) collective-permute-start(bf16[2,256,1024]{2,1,0:T(8,128)(2,1)} %get-tuple-element.778), channel_id=1, source_target_pairs={{0,1},{1,2},{2,3},{3,4},{4,5},{5,6},{6,7},{8,9},{9,10},{10,11},{11... | collective-permute-start | bytes 3145736 | tf_op jit(solution)/shard_map/while/body/eval_jaxpr/ppermute | solution.py:122
  2560.5 151.7 %collective-permute-start = (bf16[2,256,1024]{2,1,0:T(8,128)(2,1)}, bf16[2,256,1024]{2,1,0:T(8,128)(2,1)}, u32[]{:S(2)}, u32[]{:S(2)}) collective-permute-start(bf16[2,256,1024]{2,1,0:T(8,128)(2,1)} %get-tuple-element.778), channel_id=1, source_target_pairs={{0,1},{1,2},{2,3},{3,4},{4,5},{5,6},{6,7},{8,9},{9,10},{10,11},{11... | collective-permute-start | bytes 3145736 | tf_op jit(solution)/shard_map/while/body/eval_jaxpr/ppermute | solution.py:122
  2724.4 151.7 %collective-permute-start = (bf16[2,256,1024]{2,1,0:T(8,128)(2,1)}, bf16[2,256,1024]{2,1,0:T(8,128)(2,1)}, u32[]{:S(2)}, u32[]{:S(2)}) collective-permute-start(bf16[2,256,1024]{2,1,0:T(8,128)(2,1)} %get-tuple-element.778), channel_id=1, source_target_pairs={{0,1},{1,2},{2,3},{3,4},{4,5},{5,6},{6,7},{8,9},{9,10},{10,11},{11... | collective-permute-start | bytes 3145736 | tf_op jit(solution)/shard_map/while/body/eval_jaxpr/ppermute | solution.py:122
  2888.3 151.7 %collective-permute-start = (bf16[2,256,1024]{2,1,0:T(8,128)(2,1)}, bf16[2,256,1024]{2,1,0:T(8,128)(2,1)}, u32[]{:S(2)}, u32[]{:S(2)}) collective-permute-start(bf16[2,256,1024]{2,1,0:T(8,128)(2,1)} %get-tuple-element.778), channel_id=1, source_target_pairs={{0,1},{1,2},{2,3},{3,4},{4,5},{5,6},{6,7},{8,9},{9,10},{10,11},{11... | collective-permute-start | bytes 3145736 | tf_op jit(solution)/shard_map/while/body/eval_jaxpr/ppermute | solution.py:122
  3052.1 151.7 %collective-permute-start = (bf16[2,256,1024]{2,1,0:T(8,128)(2,1)}, bf16[2,256,1024]{2,1,0:T(8,128)(2,1)}, u32[]{:S(2)}, u32[]{:S(2)}) collective-permute-start(bf16[2,256,1024]{2,1,0:T(8,128)(2,1)} %get-tuple-element.778), channel_id=1, source_target_pairs={{0,1},{1,2},{2,3},{3,4},{4,5},{5,6},{6,7},{8,9},{9,10},{10,11},{11... | collective-permute-start | bytes 3145736 | tf_op jit(solution)/shard_map/while/body/eval_jaxpr/ppermute | solution.py:122
  (225 other events, 1506.1 us)
Sparse Core Ops, SparseCore 0:
  3206.9 96.0 all-reduce.1
where the time goes:
time: 3330 us; the launch traced here: 3320 us
  matrix products  1130 us (34%)
  starting transfers between devices  921 us (28%)
  waiting for transfers between devices  585 us (18%)
  other arithmetic  341 us (10%)
  local copies, waits for them, and re-layouts  262 us (8%)
  loops' own time  53.3 us (2%)
    ppermute x22, starting transfers between devices, run_tick(): recv_act = lax.ppermute(act_out, 'stage', fwd_perm)  892 us
    ppermute x22, waiting for transfers between devices, run_tick(): recv_grad = lax.ppermute(d_act, 'stage', bwd_perm)  502 us
    dot_general x8, matrix products, layer_backward(): jnp.einsum('bsf,bsd->fd', gelu_out, grad_out, preferred_element_type=jnp....  161 us
    dot_general x16, matrix products, layer_forward(): jnp.einsum('bsd,df->bsf', normed2, w_up, preferred_element_type=jnp.float32)  159 us
    dot_general x8, matrix products, layer_backward(): jnp.einsum('bsd,bsf->df', normed2, d_pre, preferred_element_type=jnp.floa...  142 us
    dot_general x16, matrix products, layer_forward(): jnp.einsum('bsd,de->bse', normed, w_qkv, preferred_element_type=jnp.float32)  106 us
    dot_general x8, matrix products, layer_backward(): jnp.einsum('bsd,fd->bsf', grad_out, w_down, preferred_element_type=jnp.fl...  98.2 us
    dot_general x8, matrix products, layer_backward(): jnp.einsum('bsf,df->bsd', d_pre, w_up, preferred_element_type=jnp.float32)  85.2 us
  transfers between devices with their start and end apart: 45, of which 7 were waited for; matrix products, arithmetic and copies ran while one was open for 35% of the time, Pallas kernels for 0%

commit v1 on v0

v1 whole, which is shorter than its diff:
```python
import functools

import jax
import jax.numpy as jnp
from jax import lax
from jax.experimental import pallas as pl
from jax.experimental.pallas import tpu as pltpu
from jax.sharding import PartitionSpec as P

F32, BF16 = jnp.float32, jnp.bfloat16
MESH = pl.DeviceIdType.MESH
NORM_EPS = 1e-6
NEG_BIG = -1e30
GELU_SCALE, GELU_CUBE = 0.7978845608028654, 0.044715


def mm(lhs, rhs):
    return jnp.dot(lhs, rhs, preferred_element_type=F32)


def mm_rt(lhs, rhs):
    return lax.dot_general(lhs, rhs, (((1,), (1,)), ((), ())), preferred_element_type=F32)


def mm_lt(lhs, rhs):
    return lax.dot_general(lhs, rhs, (((0,), (0,)), ((), ())), preferred_element_type=F32)


def inv_rms(vals):
    return lax.rsqrt(jnp.mean(vals * vals, axis=-1, keepdims=True) + NORM_EPS)


def norm_vjp(vals, d_out):
    scale = inv_rms(vals)
    return d_out * scale - vals * (scale * scale * scale * jnp.mean(vals * d_out, axis=-1, keepdims=True))


def gelu(x):
    return (0.5 * x) * (1.0 + jnp.tanh(GELU_SCALE * (x + GELU_CUBE * (x * x * x))))


def gelu_grad(x):
    x_sq = x * x
    t = jnp.tanh(GELU_SCALE * (x + GELU_CUBE * (x_sq * x)))
    return 0.5 * (1.0 + t) + (0.5 * x) * (1.0 - t * t) * (GELU_SCALE * (1.0 + (3 * GELU_CUBE) * x_sq))


def head_half(vals, which):
    lane = lax.broadcasted_iota(jnp.int32, (1, vals.shape[1]), 1)
    half = vals.shape[1] // 2
    return jnp.where((lane < half) if which == 0 else (lane >= half), vals, jnp.zeros_like(vals))


def probs(query, key, causal, scale):
    scores = (mm_rt(query, key) * scale).astype(BF16).astype(F32)
    scores = jnp.where(causal, scores, NEG_BIG)
    top = jnp.max(scores, axis=-1, keepdims=True)
    e = jnp.exp(scores - top)
    return e * (1.0 / jnp.sum(e, axis=-1, keepdims=True))


def attn_fwd(qkv, ctx, rows, width, scale):
    causal = lax.broadcasted_iota(jnp.int32, (rows, rows), 0) >= lax.broadcasted_iota(jnp.int32, (rows, rows), 1)
    for p in range(width // 128):
        q, k, v = (qkv[:, w * width + 128 * p : w * width + 128 * p + 128] for w in range(3))
        a = [probs(head_half(q, h), k, causal, scale).astype(BF16) for h in range(2)]
        both = mm(jnp.concatenate(a, 1), jnp.concatenate([head_half(v, 0), head_half(v, 1)], 0))
        ctx[:, 128 * p : 128 * p + 128] = both.astype(BF16)


def attn_bwd(qkv, d_ctx, d_qkv, rows, width, scale):
    causal = lax.broadcasted_iota(jnp.int32, (rows, rows), 0) >= lax.broadcasted_iota(jnp.int32, (rows, rows), 1)
    for p in range(width // 128):
        q, k, v = (qkv[:, w * width + 128 * p : w * width + 128 * p + 128] for w in range(3))
        d = d_ctx[:, 128 * p : 128 * p + 128]
        a_b, ds_b = [], []
        for h in range(2):
            a = probs(head_half(q, h), k, causal, scale)
            dp = mm_rt(head_half(d, h), v).astype(BF16).astype(F32)
            ds_b.append((a * (dp - jnp.sum(a * dp, axis=-1, keepdims=True))).astype(BF16))
            a_b.append(a.astype(BF16))
        split = lambda vals: jnp.concatenate([head_half(vals, 0), head_half(vals, 1)], 0)
        dq = mm(jnp.concatenate(ds_b, 1), split(k)) * scale
        dk = mm_lt(jnp.concatenate(ds_b, 0), split(q)) * scale
        dv = mm_lt(jnp.concatenate(a_b, 0), split(d))
        for w, val in enumerate((dq, dk, dv)):
            d_qkv[:, w * width + 128 * p : w * width + 128 * p + 128] = val.astype(BF16)


def pipeline_kernel(
    axis, stages, units, scale, inv_count,
    embeds, targets, w_qkv_h, w_out_h, w_up_h, w_down_h,
    xn_all, ctx_all, z_all, gl_all, dqkv_all, dh_all, dpre_all, g_all, dx_all, qkv_all, h_all, pre_all, loss,
    w_qkv, w_out, w_up, w_down, act, grad, out, d_in, target,
    xn, qkv, ctx, hid, z, pre, gl, dpre, dh, dctx, dqkv,
    w_sem, emb_sem, tgt_sem, f_send, f_recv, b_send, b_recv, f_save, b_save, b_load,
):
    stage = lax.axis_index(axis)
    last = stages - 1
    rows, width = act.shape[1], act.shape[2]
    right, left = lax.rem(stage + 1, stages), lax.rem(stage + last, stages)
    barrier = pltpu.get_barrier_semaphore()
    for neighbour in (left, right):
        pl.semaphore_signal(barrier, inc=1, device_id={axis: neighbour}, device_id_type=MESH)

    w_copies = [
        pltpu.make_async_copy(src, dst, w_sem.at[i])
        for i, (src, dst) in enumerate(((w_qkv_h, w_qkv), (w_out_h, w_out), (w_up_h, w_up), (w_down_h, w_down)))
    ]

    def embed_copy(unit):
        return pltpu.make_async_copy(embeds.at[unit], act.at[unit], emb_sem.at[unit])

    @pl.when(stage == 0)
    def _():
        embed_copy(0).start()

    for copy in w_copies:
        copy.start()

    @pl.when(stage == 0)
    def _():
        lax.fori_loop(1, units, lambda unit, c: (embed_copy(unit).start(), c)[1], 0)

    pl.semaphore_wait(barrier, 2)
    loss[...] = jnp.zeros_like(loss)

    def f_copy(unit):
        return pltpu.make_async_remote_copy(
            src_ref=out.at[lax.rem(unit, 2)], dst_ref=act.at[unit], send_sem=f_send.at[lax.rem(unit, 2)],
            recv_sem=f_recv.at[unit], device_id={axis: right}, device_id_type=MESH)

    def b_copy(unit):
        return pltpu.make_async_remote_copy(
            src_ref=d_in.at[lax.rem(unit, 2)], dst_ref=grad.at[unit], send_sem=b_send.at[lax.rem(unit, 2)],
            recv_sem=b_recv.at[unit], device_id={axis: left}, device_id_type=MESH)

    def dx_copy(unit):
        return pltpu.make_async_copy(d_in.at[lax.rem(unit, 2)], dx_all.at[unit], b_send.at[lax.rem(unit, 2)])

    def f_saves(unit):
        pairs = ((xn, xn_all), (qkv.at[0], qkv_all), (ctx, ctx_all), (hid.at[0], h_all), (z, z_all), (pre.at[0], pre_all), (gl, gl_all))
        return [pltpu.make_async_copy(src, dst.at[unit], f_save.at[i]) for i, (src, dst) in enumerate(pairs)]

    def b_saves(unit):
        pairs = ((dpre, dpre_all), (dh, dh_all), (dqkv, dqkv_all), (grad.at[unit], g_all))
        return [pltpu.make_async_copy(src, dst.at[unit], b_save.at[i]) for i, (src, dst) in enumerate(pairs)]

    def b_loads(unit):
        pairs = ((pre_all, pre.at[1]), (h_all, hid.at[1]), (qkv_all, qkv.at[1]))
        return [pltpu.make_async_copy(src.at[unit], dst, b_load.at[i]) for i, (src, dst) in enumerate(pairs)]

    def target_copy(unit):
        return pltpu.make_async_copy(targets.at[unit], target, tgt_sem)

    def forward(unit):
        slot = lax.rem(unit, 2)

        @pl.when(stage == last)
        def _():
            target_copy(unit).start()

        @pl.when(stage == 0)
        def _():
            embed_copy(unit).wait()

        @pl.when(stage > 0)
        def _():
            f_copy(unit).wait_recv()

        @pl.when(unit == 0)
        def _():
            w_copies[0].wait()

        saves = f_saves(unit)
        x = act[unit].astype(F32)
        xn[...] = (x * inv_rms(x)).astype(BF16)
        qkv[0] = mm(xn[...], w_qkv[...]).astype(BF16)
        attn_fwd(qkv.at[0], ctx, rows, width, scale)

        @pl.when(unit == 0)
        def _():
            for copy in w_copies[1:]:
                copy.wait()

        for i in range(3):
            saves[i].start()
        h = (act[unit].astype(F32) + mm(ctx[...], w_out[...])).astype(BF16)
        hid[0] = h
        h = h.astype(F32)
        z[...] = (h * inv_rms(h)).astype(BF16)
        for i in range(3, 5):
            saves[i].start()
        p = mm(z[...], w_up[...]).astype(BF16)
        pre[0] = p
        gl[...] = gelu(p.astype(F32)).astype(BF16)
        for i in range(5, 7):
            saves[i].start()

        @pl.when((stage < last) & (unit >= 2))
        def _():
            f_copy(unit).wait_send()

        out[slot] = (hid[0].astype(F32) + mm(gl[...], w_down[...])).astype(BF16)

        @pl.when(stage < last)
        def _():
            f_copy(unit).start()

        @pl.when(stage == last)
        def _():
            target_copy(unit).wait()
            err = out[slot].astype(F32) - target[...].astype(F32)
            grad[unit] = (err * inv_count).astype(BF16)
            part = jnp.sum((err * err).reshape(rows // 8, 8, width // 128, 128), axis=(0, 2))
            loss[...] += part * (0.5 * inv_count)

    def backward(unit):
        src = jnp.where(stage == last, 0, 1)
        slot = lax.rem(unit, 2)

        @pl.when(stage < last)
        def _():
            b_copy(unit).wait_recv()
            for copy in b_loads(unit):
                copy.wait()

        saves = b_saves(unit)

        @pl.when(unit > 0)
        def _():
            for copy in b_saves(unit - 1):
                copy.wait()

        saves[3].start()
        d_gelu = mm_rt(grad[unit], w_down[...]).astype(BF16).astype(F32)
        dpre[...] = (d_gelu * gelu_grad(pre[src].astype(F32))).astype(BF16)
        saves[0].start()
        dz = mm_rt(dpre[...], w_up[...]).astype(BF16).astype(F32)
        d_hid = (grad[unit].astype(F32) + norm_vjp(hid[src].astype(F32), dz)).astype(BF16)
        dh[...] = d_hid
        saves[1].start()
        dctx[...] = mm_rt(d_hid, w_out[...]).astype(BF16)
        attn_bwd(qkv.at[src], dctx, dqkv, rows, width, scale)
        saves[2].start()

        @pl.when(unit >= 2)
        def _():
            @pl.when(stage > 0)
            def _():
                b_copy(unit).wait_send()

            @pl.when(stage == 0)
            def _():
                dx_copy(unit).wait()

        du = mm_rt(dqkv[...], w_qkv[...]).astype(BF16).astype(F32)
        d_in[slot] = (dh[...].astype(F32) + norm_vjp(act[unit].astype(F32), du)).astype(BF16)

        @pl.when(stage > 0)
        def _():
            b_copy(unit).start()

        @pl.when(stage == 0)
        def _():
            dx_copy(unit).start()

    def tick(t, carry):
        f_unit = t - stage
        b_unit = t - 2 * last + stage

        @pl.when((f_unit >= 1) & (f_unit <= units))
        def _():
            for copy in f_saves(f_unit - 1):
                copy.wait()

        @pl.when((f_unit >= 0) & (f_unit < units))
        def _():
            forward(f_unit)

        @pl.when((b_unit >= 0) & (b_unit < units))
        def _():
            backward(b_unit)

        @pl.when((stage < last) & (b_unit >= -1) & (b_unit < units - 1))
        def _():
            for copy in b_loads(b_unit + 1):
                copy.start()

        return carry

    lax.fori_loop(0, units + 2 * last, tick, 0)

    for copy in b_saves(units - 1):
        copy.wait()

    for unit in (units - 2, units - 1):
        @pl.when(stage < last)
        def _():
            f_copy(unit).wait_send()

        @pl.when(stage > 0)
        def _():
            b_copy(unit).wait_send()

        @pl.when(stage == 0)
        def _():
            dx_copy(unit).wait()


def run_pipeline(axis, stages, embeds, targets, w_qkv, w_out, w_up, w_down, head_dim):
    units, rows, width = embeds.shape
    ff = w_up.shape[1]
    act_t = lambda n: jax.ShapeDtypeStruct((units, rows, n), BF16)
    hbm = pl.BlockSpec(memory_space=pl.ANY)
    row_t = lambda *shape: pltpu.VMEM(shape, BF16)
    dma = pltpu.SemaphoreType.DMA
    outs = [act_t(n) for n in (width, width, width, ff, 3 * width, width, ff, width, width, 3 * width, width, ff)]
    outs.append(jax.ShapeDtypeStruct((8, 128), F32))
    return pl.pallas_call(
        functools.partial(pipeline_kernel, axis, stages, units, head_dim ** -0.5, 1.0 / (units * rows * width)),
        out_shape=outs,
        in_specs=[hbm] * 6,
        out_specs=[hbm] * 12 + [pl.BlockSpec(memory_space=pltpu.VMEM)],
        scratch_shapes=[
            row_t(*w_qkv.shape), row_t(*w_out.shape), row_t(*w_up.shape), row_t(*w_down.shape),
            row_t(units, rows, width), row_t(units, rows, width), row_t(2, rows, width), row_t(2, rows, width), row_t(rows, width),
            row_t(rows, width), row_t(2, rows, 3 * width), row_t(rows, width), row_t(2, rows, width), row_t(rows, width),
            row_t(2, rows, ff), row_t(rows, ff), row_t(rows, ff), row_t(rows, width), row_t(rows, width), row_t(rows, 3 * width),
            dma((4,)), dma((units,)), dma, dma((2,)), dma((units,)), dma((2,)), dma((units,)), dma((7,)), dma((4,)), dma((3,)),
        ],
        compiler_params=pltpu.CompilerParams(collective_id=0, has_side_effects=True, vmem_limit_bytes=67043328),
        name="pipeline",
    )(embeds, targets, w_qkv, w_out, w_up, w_down)


def solution(mesh):
    num_stages = mesh.shape["stage"]

    def stage_program(embeds, targets, w_qkv, w_out, w_up, w_down):
        num_micro, batch_size, seq_len, model_dim = embeds.shape
        num_heads, head_dim = w_out.shape[1], w_out.shape[2]
        flat = (num_micro * batch_size, seq_len, model_dim)
        res = run_pipeline(
            "stage", num_stages, embeds.reshape(flat), targets.reshape(flat),
            w_qkv[0], w_out[0].reshape(num_heads * head_dim, model_dim), w_up[0], w_down[0], head_dim)
        xn, ctx, z, gl, dqkv, dh, dpre, g, dx = res[:9]
        loss = res[-1]
        grad_w = lambda a, b: jnp.einsum("usd,use->de", a, b, preferred_element_type=F32)
        is_first = lax.axis_index("stage") == 0
        is_last = lax.axis_index("stage") == num_stages - 1
        dx = lax.psum(jnp.where(is_first, dx, jnp.zeros_like(dx)), "stage")
        total = lax.psum(jnp.where(is_last, jnp.sum(loss), 0.0), "stage").reshape(1)
        return (
            total,
            grad_w(xn, dqkv)[None],
            grad_w(ctx, dh).reshape(w_out.shape),
            grad_w(z, dpre)[None],
            grad_w(gl, g)[None],
            dx.reshape(embeds.shape),
        )

    act_spec = P("rep", None, None, None)
    w3_spec = P("stage", None, None)
    g3_spec = P(("rep", "stage"), None, None)
    in_specs = (act_spec, act_spec, w3_spec, P("stage", None, None, None), w3_spec, w3_spec)
    out_specs = (P("rep"), g3_spec, P(("rep", "stage"), None, None, None), g3_spec, g3_spec, act_spec)
    return jax.shard_map(stage_program, mesh=mesh, in_specs=in_specs, out_specs=out_specs, check_vma=False)
```

time: 3330 us -> 892 us (0.27)
  matrix products: 1130 us -> 137 us
  starting transfers between devices: 921 us -> 0.06 us
  Pallas kernels: 0 us -> 694 us
  waiting for transfers between devices: 585 us -> 0.06 us
  other arithmetic: 341 us -> 7.93 us
  local copies, waits for them, and re-layouts: 262 us -> 8.75 us
  loops' own time: 53.3 us -> 0 us
    dot_general x176 -> x4, matrix products: 1130 us -> 137 us  [stage_program(): jnp.einsum('usd,use->de', a, b, preferred_element_type=F32)]
    ppermute x44 -> x0, starting transfers between devices: 921 us -> none  [the longest x22 892 us: run_tick(): recv_act = lax.ppermute(act_out, 'stage', fwd_perm)]
    pallas_call x0 -> x1, Pallas kernels: none -> 694 us  [run_pipeline(): pl.pallas_call(functools.partial(pipeline_kernel, axis, stages, units, he...]
    ppermute x44 -> x0, waiting for transfers between devices: 502 us -> none  [the longest x22 502 us: run_tick(): recv_grad = lax.ppermute(d_act, 'stage', bwd_perm)]
    dynamic_update_slice x44 -> x0, other arithmetic: 111 us -> none  [the longest x22 70.6 us: run_tick(): lax.dynamic_update_index_in_dim(saved_inputs, jnp.where(fwd_ok, layer_in,...]
    psum x1, waiting for transfers between devices: 82.4 us -> 0.01 us  [stage_program(): dx = lax.psum(jnp.where(is_first, dx, jnp.zeros_like(dx)), 'stage')]
    reduce_sum x38 -> x1, other arithmetic: 82.8 us -> 0.6 us  [stage_program(): total = lax.psum(jnp.where(is_last, jnp.sum(loss), 0.0), 'stage').reshape(1)]
    broadcast_in_dim x48 -> x0, local copies, waits for them, and re-layouts: 82 us -> none  [the longest x44 56.5 us: stage_program(): zero_act = jnp.zeros((batch_size, seq_len, model_dim), jnp.bfloat16)]
  transfers between devices with their start and end apart: 45 -> 1, of which waited for: 7 -> 0; matrix products, arithmetic and copies ran while one was open for 35% -> 16% of each run, Pallas kernels for 0% -> 0%
where the time goes in v1:
time: 892 us; the launch traced here: 876 us
  Pallas kernels  694 us (78%)
  matrix products  137 us (15%)
  between operations  15.2 us (2%)
  blocking collectives  13.8 us (2%)
    pallas_call x1, Pallas kernels, run_pipeline(): pl.pallas_call(functools.partial(pipeline_kernel, axis, stages, units, he...  694 us
    dot_general x4, matrix products, stage_program(): jnp.einsum('usd,use->de', a, b, preferred_element_type=F32)  137 us
  transfers between devices with their start and end apart: 1, of which 0 were waited for; matrix products, arithmetic and copies ran while one was open for 16% of the time, Pallas kernels for 0%

profile of v1, /device:TPU:112, one launch (start us, length us, event | category | flops | bytes accessed | tf_op | source)
XLA Modules:
  0.0 876.0 jit_solution(13465264787695537535)
XLA Ops:
  7.2 0.1 all-reduce.2.cloned.1.call-start
  7.3 693.5 %pipeline.1 = (bf16[16,256,1024]{2,1,0:T(8,128)(2,1)}, bf16[16,256,1024]{2,1,0:T(8,128)(2,1)}, bf16[16,256,1024]{2,1,0:T(8,128)(2,1)}, bf16[16,256,4096]{2,1,0:T...) custom-call(bf16[16,256,1024]{2,1,0:T(8,128)(2,1)} %bitcast.29, ...), custom_call_target="tpu_custom_call" | custom-call | tf_op jit(solution)/shard_map/pipeline/pallas_call | solution.py:320
  700.8 7.3 broadcast_select_fusion
  708.1 0.0 copy-start
  708.1 0.1 all-reduce.2.cloned.1.call-update
  708.2 0.6 copy-done
  708.8 0.6 reduce_sum.9
  710.0 13.8 %psum.14 = f32[1]{0:T(128)} all-reduce(f32[1]{0:T(128)} %bitcast.6), channel_id=1, replica_groups=mesh['rep'=2,'stage'=8] {'stage'}, use_global_device_ids=true, to_apply=%region_1.2 | all-reduce | flops 1 | bytes 8 | tf_op jit(solution)/shard_map/psum | solution.py:353
  723.8 43.6 %convolution_bitcast_fusion = f32[1,4096,1024]{2,1,0:T(8,128)} fusion(bf16[16,256,4096]{2,1,0:T(8,128)(2,1)} %get-tuple-element.23, bf16[16,256,1024]{2,1,0:T(8,128)(2,1)} %get-tuple-element.24), kind=kOutput, calls=%fused_computation | convolution fusion | flops 34359738368 | bytes 58720256 | tf_op jit(solution)/shard_map/usd,use->de/dot_general | solution.py:349
  767.4 0.0 slice-start
  767.4 15.2 %fusion = f32[1024,1024,1]{1,0,2:T(8,128)} fusion(bf16[16,256,1024]{2,1,0:T(8,128)(2,1)} %get-tuple-element.19, bf16[16,256,1024]{2,1,0:T(8,128)(2,1)} %get-tuple-element.20), kind=kOutput, calls=%fused_computation.4 | convolution fusion | flops 8589934592 | bytes 20971520 | tf_op jit(solution)/shard_map/usd,use->de/dot_general | solution.py:349
  782.6 0.0 slice-start.1
  782.6 35.4 %convolution_bitcast_fusion.2 = f32[1,1024,3072]{2,1,0:T(8,128)} fusion(bf16[16,256,1024]{2,1,0:T(8,128)(2,1)} %get-tuple-element.17, bf16[16,256,3072]{2,1,0:T(8,128)(2,1)} %get-tuple-element.18), kind=kOutput, calls=%fused_computation.3 | convolution fusion | flops 25769803776 | bytes 46137344 | tf_op jit(solution)/shard_map/usd,use->de/dot_general | solution.py:349
  818.0 0.0 slice-done
  818.0 0.0 slice-done.1
  818.0 42.6 %convolution_bitcast_fusion.1 = f32[1,1024,4096]{2,1,0:T(8,128)} fusion(bf16[16,256,1024]{2,1,0:T(8,128)(2,1)S(1)} %bitcast.36, bf16[16,256,4096]{2,1,0:T(8,128)(2,1)} %get-tuple-element.22), kind=kOutput, calls=%fused_computation.1 | convolution fusion | flops 34359738368 | bytes 58720256 | tf_op jit(solution)/shard_map/usd,use->de/dot_general | solution.py:349
  860.6 0.0 all-reduce.2.cloned.1.call-done
  860.6 8.1 copy.21
  (1 shorter events, 0.0 us)
Async XLA Ops:
  7.2 853.4 %all-reduce.2.cloned.1.call-start = ((), (), s32[]{:S(2)}) async-start(), calls=%async_computation | async-start | bytes 16777216 | tf_op jit(solution)/shard_map/psum | solution.py:352
  708.1 0.7 copy-start
  767.4 50.5 %slice-start = ((s8[8388608]{0:T(1024)(128)(4,1)}), s8[4194304]{0:T(1024)(128)(4,1)S(1)}, s32[]{:S(2)}) async-start(s8[8388608]{0:T(1024)(128)(4,1)} %bitcast.35), calls=%async_computation.1 | async-start | bytes 8388608
  782.6 35.4 %slice-start.1 = ((s8[8388608]{0:T(1024)(128)(4,1)}), s8[4194304]{0:T(1024)(128)(4,1)S(1)}, s32[]{:S(2)}) async-start(s8[8388608]{0:T(1024)(128)(4,1)} %bitcast.35), calls=%async_computation.2 | async-start | bytes 8388608
Sparse Core Ops, SparseCore 0:
  708.3 95.9 all-reduce.1

commit v2 on v1

v2 whole, which is shorter than its diff:
```python
import functools

import jax
import jax.numpy as jnp
from jax import lax
from jax.experimental import pallas as pl
from jax.experimental.pallas import tpu as pltpu
from jax.sharding import PartitionSpec as P


F32, BF16 = jnp.float32, jnp.bfloat16
MESH = pl.DeviceIdType.MESH
NORM_EPS = 1e-6
NEG_BIG = -1e30
GELU_SCALE, GELU_CUBE = 0.7978845608028654, 0.044715
LANE = 128
NORM_ROWS = 32
RING = 4
VMEM_BYTES = 67043328


def mm(lhs, rhs):
    return jnp.dot(lhs, rhs, preferred_element_type=F32)


def mm_rt(lhs, rhs):
    return lax.dot_general(lhs, rhs, (((1,), (1,)), ((), ())), preferred_element_type=F32)


def mm_lt(lhs, rhs):
    return lax.dot_general(lhs, rhs, (((0,), (0,)), ((), ())), preferred_element_type=F32)


def cols(ref, lo, hi):
    return jnp.concatenate([ref[j] for j in range(lo, hi)], 1)


def rows_of(ref, lo, hi):
    return jnp.concatenate([ref[j, lo:hi, :] for j in range(ref.shape[0])], 1)


def pieces(vals):
    return [vals[:, LANE * j : LANE * j + LANE] for j in range(vals.shape[1] // LANE)]


def put(ref, lo, vals):
    for j, piece in enumerate(pieces(vals)):
        ref[lo + j] = piece


def accumulate(ref, vals, first):
    for j, piece in enumerate(pieces(vals)):
        ref[j] = piece if first else ref[j] + piece


def transpose_into(dst, src, lo, hi):
    for j in range(lo, hi):
        flipped = src[j].T
        for t, piece in enumerate(pieces(flipped)):
            dst[t, LANE * j : LANE * j + LANE, :] = piece


def row_scale(sums, width):
    return jnp.sum(sums, axis=-1, keepdims=True) * (1.0 / width)


def norm_into(dst, load):
    blocks, height = dst.shape[0], dst.shape[1]
    for r in range(0, height, NORM_ROWS):
        vals = [load(j, r) for j in range(blocks)]
        total = sum(v * v for v in vals)
        scale = lax.rsqrt(row_scale(total, blocks * LANE) + NORM_EPS)
        for j, v in enumerate(vals):
            dst[j, r : r + NORM_ROWS, :] = (v * scale).astype(BF16)


def norm_vjp_into(dst, base, load, d_load):
    blocks, height = dst.shape[0], dst.shape[1]
    width = blocks * LANE
    for r in range(0, height, NORM_ROWS):
        vals = [load(j, r) for j in range(blocks)]
        grads = [d_load(j, r) for j in range(blocks)]
        scale = lax.rsqrt(row_scale(sum(v * v for v in vals), width) + NORM_EPS)
        pull = scale * scale * scale * row_scale(sum(v * d for v, d in zip(vals, grads)), width)
        for j in range(blocks):
            dst[j, r : r + NORM_ROWS, :] = (base(j, r) + (grads[j] * scale - vals[j] * pull)).astype(BF16)


def reader(ref):
    return lambda j, r: ref[j, r : r + NORM_ROWS, :].astype(F32)


def rounded(ref):
    return lambda j, r: ref[j, r : r + NORM_ROWS, :].astype(BF16).astype(F32)


def gelu(x):
    t = jnp.tanh(x * (GELU_SCALE + (GELU_SCALE * GELU_CUBE) * (x * x)))
    return (0.5 * x) * (1.0 + t)


def gelu_grad(x):
    x_sq = x * x
    t = jnp.tanh(x * (GELU_SCALE + (GELU_SCALE * GELU_CUBE) * x_sq))
    up = 1.0 + t
    return 0.5 * (up + (((1.0 - t) * up) * x) * (GELU_SCALE + (3 * GELU_SCALE * GELU_CUBE) * x_sq))


def head_half(vals, which):
    lane = lax.broadcasted_iota(jnp.int32, (1, LANE), 1)
    return jnp.where((lane < LANE // 2) if which == 0 else (lane >= LANE // 2), vals, jnp.zeros_like(vals))


def split_heads(vals):
    return [head_half(vals, 0), head_half(vals, 1)]


def pair_scores(keys, queries):
    n = LANE
    return mm_rt(keys[:n], queries[:n]), mm_rt(keys, queries[n:])


def column_softmax(scores):
    e = jnp.exp(scores - jnp.max(scores, axis=0, keepdims=True))
    return e * (1.0 / jnp.sum(e, axis=0, keepdims=True))


def probs(scores, causal, scale):
    n = LANE
    s0, s1 = ((s * scale).astype(BF16).astype(F32) for s in scores)
    s0 = jnp.where(causal, s0, NEG_BIG)
    s1 = jnp.concatenate([s1[:n], jnp.where(causal, s1[n:], NEG_BIG)], 0)
    return column_softmax(s0), column_softmax(s1)


def causal_mask():
    return lax.broadcasted_iota(jnp.int32, (LANE, LANE), 0) <= lax.broadcasted_iota(jnp.int32, (LANE, LANE), 1)


def layer_forward(x, w_qkv, w_out, w_up, w_down, u, qkv, ctx_t, hid, pre, gl, out, acc, u_t, z_t, gl_t, scale, marks):
    blocks = x.shape[0]
    ff_blocks = w_up.shape[0]
    quads = blocks // 2
    half = LANE // 2
    causal = causal_mask()
    norm_into(u, reader(x))

    def project(i):
        for w in range(3):
            lo = w * blocks + 2 * i
            put(qkv, lo, mm(cols(u, 0, blocks), cols(w_qkv, lo, lo + 2)).astype(BF16))

    def out_part(lo, hi):
        return mm_lt(jnp.concatenate([ctx_t[0, lo:hi, :], ctx_t[1, lo:hi, :]], 1), rows_of(w_out, lo, hi))

    project(0)
    transpose_into(u_t, u, 0, blocks)
    for i in range(quads):
        pairs = (2 * i, 2 * i + 1)
        scores = [pair_scores(k, qkv[p]) for p in pairs for k in split_heads(qkv[blocks + p])]
        if i < quads - 1:
            project(i + 1)
        else:
            marks["qkv"]()
            accumulate(acc, out_part(0, 2 * LANE * i), True)
        a = [probs(s, causal, scale) for s in scores]
        for j, p in enumerate(pairs):
            v_t = qkv[2 * blocks + p].T
            for h in range(2):
                a0, a1 = a[2 * j + h]
                rows = slice(LANE * p + half * h, LANE * p + half * h + half)
                v_head = v_t[half * h : half * h + half]
                ctx_t[0, rows, :] = mm(v_head[:, :LANE], a0.astype(BF16)).astype(BF16)
                ctx_t[1, rows, :] = mm(v_head, a1.astype(BF16)).astype(BF16)
    accumulate(acc, out_part(2 * LANE * (quads - 1), blocks * LANE), False)
    marks["ctx"]()
    for r in range(0, x.shape[1], NORM_ROWS):
        for j in range(blocks):
            hid[j, r : r + NORM_ROWS, :] = (x[j, r : r + NORM_ROWS, :].astype(F32) + acc[j, r : r + NORM_ROWS, :]).astype(BF16)
    norm_into(u, reader(hid))
    step = 4
    up = lambda c: mm(cols(u, 0, blocks), cols(w_up, c, c + step)).astype(BF16)
    cur = up(0)
    transpose_into(z_t, u, 0, blocks)
    for c in range(0, ff_blocks, step):
        nxt = up(c + step) if c + step < ff_blocks else None
        for j, piece in enumerate(pieces(cur)):
            pre[c + j] = piece
            gl[c + j] = gelu(piece.astype(F32)).astype(BF16)
        transpose_into(gl_t, gl, c, c + step)
        cur = nxt
    marks["ff"]()
    for j, piece in enumerate(pieces(mm(cols(gl, 0, ff_blocks), cols(w_down, 0, blocks)))):
        out[j] = (hid[j].astype(F32) + piece).astype(BF16)


def layer_backward(g, x, hid, qkv, pre, w_qkv, w_out, w_up, w_down, d_qkv, d_ctx, d_hid, d_pre, out, acc, scale, marks):
    blocks = x.shape[0]
    ff_blocks = w_up.shape[0]
    quads = blocks // 2
    half = LANE // 2
    causal = causal_mask()
    step = 4
    down = lambda c: mm_rt(cols(g, 0, blocks), rows_of(w_down, LANE * c, LANE * (c + step))).astype(BF16)
    cur = down(0)
    for c in range(0, ff_blocks, step):
        nxt = down(c + step) if c + step < ff_blocks else None
        for j, piece in enumerate(pieces(cur)):
            d_pre[c + j] = (piece.astype(F32) * gelu_grad(pre[c + j].astype(F32))).astype(BF16)
        accumulate(acc, mm_rt(cols(d_pre, c, c + step), cols(w_up, c, c + step)), c == 0)
        cur = nxt
    norm_vjp_into(d_hid, reader(g), reader(hid), rounded(acc))
    marks["ff"]()

    def ctx_part(i):
        put(d_ctx, 2 * i, mm_rt(cols(d_hid, 0, blocks), rows_of(w_out, 2 * LANE * i, 2 * LANE * (i + 1))).astype(BF16))

    def qkv_part(i):
        take = lambda ref: jnp.concatenate([ref[w * blocks + 2 * i + t] for w in range(3) for t in range(2)], 1)
        accumulate(acc, mm_rt(take(d_qkv), take(w_qkv)), i == 0)

    ctx_part(0)
    for i in range(quads):
        pairs = (2 * i, 2 * i + 1)
        scores = [pair_scores(k, qkv[p]) for p in pairs for k in split_heads(qkv[blocks + p])]
        d_probs = [pair_scores(v, d_ctx[p]) for p in pairs for v in split_heads(qkv[2 * blocks + p])]
        if i < quads - 1:
            ctx_part(i + 1)
        if i > 0:
            qkv_part(i - 1)
        a, ds = [], []
        for s, dp in zip(scores, d_probs):
            a_pair = probs(s, causal, scale)
            dp = [d.astype(BF16).astype(F32) for d in dp]
            ds.append([(p * (d - jnp.sum(p * d, axis=0, keepdims=True))).astype(BF16) for p, d in zip(a_pair, dp)])
            a.append([p.astype(BF16) for p in a_pair])
        for j, p in enumerate(pairs):
            n = LANE

            def weigh(first, second, vals):
                top = mm(
                    jnp.concatenate([first[0], first[1][:n], second[0], second[1][:n]], 1), jnp.concatenate(vals, 0))
                low = mm(
                    jnp.concatenate([first[1][n:], second[1][n:]], 1), jnp.concatenate([vals[0][n:], vals[1][n:]], 0))
                return jnp.concatenate([top, low], 0)

            heads = (2 * j, 2 * j + 1)
            d_qkv[2 * blocks + p] = weigh(*(a[h] for h in heads), split_heads(d_ctx[p])).astype(BF16)
            d_qkv[blocks + p] = (weigh(*(ds[h] for h in heads), split_heads(qkv[p])) * scale).astype(BF16)
            k_t = qkv[blocks + p].T
            dq_t = []
            for h in range(2):
                k_head = k_t[half * h : half * h + half]
                d0, d1 = ds[heads[h]]
                dq_t.append(jnp.concatenate([mm(k_head[:, :n], d0), mm(k_head, d1)], 1) * scale)
            d_qkv[p] = jnp.concatenate(dq_t, 0).astype(BF16).T
    qkv_part(quads - 1)
    marks["qkv"]()
    norm_vjp_into(out, reader(d_hid), reader(x), rounded(acc))


def pipeline_kernel(
    axis, stages, units, scale, inv_count,
    embeds, targets, w_qkv_h, w_out_h, w_up_h, w_down_h,
    ut_all, ctx_all, zt_all, glt_all, dqkv_all, dh_all, dpre_all, g_all, dx_all, qkv_all, h_all, pre_all, x_all, loss,
    w_qkv, w_out, w_up, w_down, act, grad, out, d_in, target,
    u, qkv, ctx_t, hid, pre, gl, u_t, z_t, gl_t, acc, dpre, dh, dctx, dqkv,
    w_sem, emb_sem, tgt_sem, f_send, f_recv, f_free, b_send, b_recv, b_free, f_save, b_save, b_load,
):
    stage = lax.axis_index(axis)
    last = stages - 1
    blocks, height = act.shape[1], act.shape[2]
    right, left = lax.rem(stage + 1, stages), lax.rem(stage + last, stages)
    barrier = pltpu.get_barrier_semaphore()
    for neighbour in (left, right):
        pl.semaphore_signal(barrier, inc=1, device_id={axis: neighbour}, device_id_type=MESH)

    def load_columns(src, dst, sem):
        def start(j, carry):
            pltpu.make_async_copy(src.at[:, pl.ds(pl.multiple_of(j * LANE, LANE), LANE)], dst.at[j], sem).start()
            return carry

        lax.fori_loop(0, dst.shape[0], start, 0)

    def wait_whole(ref, sem):
        pltpu.make_async_copy(ref, ref, sem).wait()

    def embed_slot(unit):
        return act.at[lax.rem(unit, RING)], emb_sem.at[lax.rem(unit, RING)]

    def embed_start(unit):
        load_columns(embeds.at[unit], *embed_slot(unit))

    weights = ((w_qkv_h, w_qkv), (w_out_h, w_out), (w_up_h, w_up), (w_down_h, w_down))

    @pl.when(stage == 0)
    def _():
        embed_start(0)

    for i, (src, dst) in enumerate(weights):
        load_columns(src, dst, w_sem.at[i])

    @pl.when(stage == 0)
    def _():
        embed_start(1)

    pl.semaphore_wait(barrier, 2)
    loss[...] = jnp.zeros_like(loss)

    def f_copy(unit):
        slot, ring = lax.rem(unit, 2), lax.rem(unit, RING)
        return pltpu.make_async_remote_copy(
            src_ref=out.at[slot], dst_ref=act.at[ring], send_sem=f_send.at[slot], recv_sem=f_recv.at[ring],
            device_id={axis: right}, device_id_type=MESH)

    def b_copy(unit):
        slot, ring = lax.rem(unit, 2), lax.rem(unit, RING)
        return pltpu.make_async_remote_copy(
            src_ref=d_in.at[slot], dst_ref=grad.at[ring], send_sem=b_send.at[slot], recv_sem=b_recv.at[ring],
            device_id={axis: left}, device_id_type=MESH)

    def dx_copy(unit):
        slot = lax.rem(unit, 2)
        return pltpu.make_async_copy(d_in.at[slot], dx_all.at[unit], b_send.at[slot])

    def f_saves(unit):
        pairs = (
            (act.at[lax.rem(unit, RING)], x_all), (u_t, ut_all), (qkv.at[0], qkv_all), (ctx_t, ctx_all),
            (hid.at[0], h_all), (z_t, zt_all), (pre.at[0], pre_all), (gl_t, glt_all))
        return [pltpu.make_async_copy(src, dst.at[unit], f_save.at[i]) for i, (src, dst) in enumerate(pairs)]

    def b_saves(unit):
        pairs = ((grad.at[lax.rem(unit, RING)], g_all), (dpre, dpre_all), (dh, dh_all), (dqkv, dqkv_all))
        return [pltpu.make_async_copy(src, dst.at[unit], b_save.at[i]) for i, (src, dst) in enumerate(pairs)]

    def b_loads(unit):
        pairs = (
            (pre_all, pre.at[1]), (h_all, hid.at[1]), (qkv_all, qkv.at[1]), (x_all, act.at[RING + lax.rem(unit, 2)]))
        return [pltpu.make_async_copy(src.at[unit], dst, b_load.at[i]) for i, (src, dst) in enumerate(pairs)]

    def forward(unit):
        ring, slot = lax.rem(unit, RING), lax.rem(unit, 2)
        saves = f_saves(unit)

        @pl.when(stage == last)
        def _():
            load_columns(targets.at[unit], target, tgt_sem)

        @pl.when((stage == 0) & (unit + 2 < units))
        def _():
            embed_start(unit + 2)

        @pl.when(stage == 0)
        def _():
            wait_whole(*embed_slot(unit))

        @pl.when(stage > 0)
        def _():
            f_copy(unit).wait_recv()

        @pl.when(unit == 0)
        def _():
            wait_whole(w_qkv, w_sem.at[0])

        saves[0].start()

        def qkv_ready():
            @pl.when(unit == 0)
            def _():
                wait_whole(w_out, w_sem.at[1])

            saves[1].start()
            saves[2].start()

        def ctx_ready():
            @pl.when(unit == 0)
            def _():
                wait_whole(w_up, w_sem.at[2])
                wait_whole(w_down, w_sem.at[3])

            saves[3].start()

        def ff_ready():
            for i in range(4, 8):
                saves[i].start()

            @pl.when((stage < last) & (unit >= 2))
            def _():
                f_copy(unit).wait_send()

            @pl.when((stage < last) & (unit >= RING))
            def _():
                pl.semaphore_wait(f_free, 1)

        layer_forward(
            act.at[ring], w_qkv, w_out, w_up, w_down, u, qkv.at[0], ctx_t, hid.at[0], pre.at[0], gl, out.at[slot], acc,
            u_t, z_t, gl_t, scale, {"qkv": qkv_ready, "ctx": ctx_ready, "ff": ff_ready})

        @pl.when(stage < last)
        def _():
            f_copy(unit).start()

        @pl.when(stage == last)
        def _():
            wait_whole(target, tgt_sem)
            part = jnp.zeros((8, LANE), F32)
            for j in range(blocks):
                err = out[slot, j].astype(F32) - target[j].astype(F32)
                grad[ring, j] = (err * inv_count).astype(BF16)
                part += jnp.sum((err * err).reshape(height // 8, 8, LANE), axis=0)
            loss[...] += part * (0.5 * inv_count)

    def backward(unit):
        ring, slot = lax.rem(unit, RING), lax.rem(unit, 2)
        src = jnp.where(stage == last, 0, 1)
        x_slot = jnp.where(stage == last, ring, RING + slot)
        saves = b_saves(unit)
        following = b_loads(unit + 1)
        more = (stage < last) & (unit + 1 < units)

        @pl.when(unit > 0)
        def _():
            for copy in b_saves(unit - 1):
                copy.wait()

            @pl.when((stage < last) & (unit - 1 < units - RING))
            def _():
                pl.semaphore_signal(b_free, inc=1, device_id={axis: right}, device_id_type=MESH)

        @pl.when(stage < last)
        def _():
            b_copy(unit).wait_recv()
            for copy in b_loads(unit):
                copy.wait()

        saves[0].start()

        def ff_ready():
            saves[1].start()
            saves[2].start()

            @pl.when(more)
            def _():
                for i in (0, 1, 3):
                    following[i].start()

        def qkv_ready():
            saves[3].start()

            @pl.when(more)
            def _():
                following[2].start()

            @pl.when(unit >= 2)
            def _():
                @pl.when(stage > 0)
                def _():
                    b_copy(unit).wait_send()

                @pl.when(stage == 0)
                def _():
                    dx_copy(unit).wait()

            @pl.when((stage > 0) & (unit >= RING))
            def _():
                pl.semaphore_wait(b_free, 1)

        layer_backward(
            grad.at[ring], act.at[x_slot], hid.at[src], qkv.at[src], pre.at[src], w_qkv, w_out, w_up, w_down,
            dqkv, dctx, dh, dpre, d_in.at[slot], acc, scale, {"ff": ff_ready, "qkv": qkv_ready})

        @pl.when(stage > 0)
        def _():
            b_copy(unit).start()

        @pl.when(stage == 0)
        def _():
            dx_copy(unit).start()

    def tick(t, carry):
        f_unit = t - stage
        b_unit = t - 2 * last + stage

        @pl.when((f_unit >= 1) & (f_unit <= units))
        def _():
            for copy in f_saves(f_unit - 1):
                copy.wait()

            @pl.when((stage > 0) & (f_unit - 1 < units - RING))
            def _():
                pl.semaphore_signal(f_free, inc=1, device_id={axis: left}, device_id_type=MESH)

        @pl.when((stage < last) & (b_unit == 0))
        def _():
            for copy in b_loads(0):
                copy.start()

        @pl.when((f_unit >= 0) & (f_unit < units))
        def _():
            forward(f_unit)

        @pl.when((b_unit >= 0) & (b_unit < units))
        def _():
            backward(b_unit)

        return carry

    lax.fori_loop(0, units + 2 * last, tick, 0)

    for copy in b_saves(units - 1):
        copy.wait()

    for unit in (units - 2, units - 1):
        @pl.when(stage < last)
        def _():
            f_copy(unit).wait_send()

        @pl.when(stage > 0)
        def _():
            b_copy(unit).wait_send()

        @pl.when(stage == 0)
        def _():
            dx_copy(unit).wait()


def run_pipeline(axis, stages, embeds, targets, w_qkv, w_out, w_up, w_down, head_dim):
    units, height, width = embeds.shape
    n, ff = width // LANE, w_up.shape[1] // LANE
    halves = height // LANE
    saved = lambda *shape: jax.ShapeDtypeStruct((units,) + shape, BF16)
    rows_t = lambda k: saved(k, height, LANE)
    cols_t = lambda k: saved(halves, k, LANE)
    hbm = pl.BlockSpec(memory_space=pl.ANY)
    vm = lambda *shape: pltpu.VMEM(shape, BF16)
    rows = lambda *lead: vm(*lead, height, LANE)
    dma = pltpu.SemaphoreType.DMA
    outs = [
        cols_t(width), cols_t(width), cols_t(width), cols_t(ff * LANE), rows_t(3 * n), rows_t(n), rows_t(ff), rows_t(n), rows_t(n),
        rows_t(3 * n), rows_t(n), rows_t(ff), rows_t(n), jax.ShapeDtypeStruct((8, LANE), F32)]
    return pl.pallas_call(
        functools.partial(pipeline_kernel, axis, stages, units, head_dim ** -0.5, 1.0 / (units * height * width)),
        out_shape=outs,
        in_specs=[hbm] * 6,
        out_specs=[hbm] * 13 + [pl.BlockSpec(memory_space=pltpu.VMEM)],
        scratch_shapes=[
            vm(3 * n, width, LANE), vm(n, width, LANE), vm(ff, width, LANE), vm(n, ff * LANE, LANE),
            rows(RING + 2, n), rows(RING, n), rows(2, n), rows(2, n), rows(n),
            rows(n), rows(2, 3 * n), vm(halves, width, LANE), rows(2, n), rows(2, ff), rows(ff),
            vm(halves, width, LANE), vm(halves, width, LANE), vm(halves, ff * LANE, LANE),
            pltpu.VMEM((n, height, LANE), F32), rows(ff), rows(n), rows(n), rows(3 * n),
            dma((4,)), dma((RING,)), dma, dma((2,)), dma((RING,)), pltpu.SemaphoreType.REGULAR,
            dma((2,)), dma((RING,)), pltpu.SemaphoreType.REGULAR, dma((8,)), dma((4,)), dma((4,)),
        ],
        compiler_params=pltpu.CompilerParams(collective_id=0, has_side_effects=True, vmem_limit_bytes=VMEM_BYTES),
        name="pipeline",
    )(embeds, targets, w_qkv, w_out, w_up, w_down)


TILE_M, TILE_N = 1024, 512


def weight_kernel(left_refs, right_refs, out_refs, lefts, rights, tiles, l_sem, r_sem, o_sem):
    plan, left_plan = [], []
    for w, (a, b) in enumerate(zip(left_refs, right_refs)):
        m_tiles, n_tiles = a.shape[2] // TILE_M, b.shape[1] * LANE // TILE_N
        for m in range(m_tiles):
            left_plan.append((w, m, len(plan)))
            plan += [(w, m, n) for n in range(n_tiles)]
    steps, per = len(plan), TILE_N // LANE

    def left_copy(i):
        w, m, _ = left_plan[i]
        return pltpu.make_async_copy(left_refs[w].at[:, :, pl.ds(m * TILE_M, TILE_M), :], lefts.at[i % 2], l_sem.at[i % 2])

    spans = []
    for w, m, first in left_plan:
        spans.append((w, m, first, sum(1 for p in plan if p[:2] == (w, m))))

    def right_copy(step):
        for w, m, first, count in spans:
            @pl.when((step >= first) & (step < first + count))
            def _():
                slot = lax.rem(step, 2)
                pltpu.make_async_copy(
                    right_refs[w].at[:, pl.ds((step - first) * per, per)], rights.at[slot], r_sem.at[slot]).start()

    def out_copy(step):
        for w, m, first, count in spans:
            @pl.when((step >= first) & (step < first + count))
            def _():
                slot = lax.rem(step, 2)
                at = pl.multiple_of((step - first) * TILE_N, TILE_N)
                pltpu.make_async_copy(
                    tiles.at[slot], out_refs[w].at[pl.ds(m * TILE_M, TILE_M), pl.ds(at, TILE_N)], o_sem.at[slot]).start()

    def wait_out(slot):
        pltpu.make_async_copy(tiles.at[slot], tiles.at[slot], o_sem.at[slot]).wait()

    left_copy(0).start()
    right_copy(0)
    left_copy(1).start()

    def body(step, phase):
        slot = lax.rem(step, 2)

        @pl.when(step + 1 < steps)
        def _():
            right_copy(step + 1)

        fresh = functools.reduce(jnp.logical_or, [step == first for _, _, first, _ in spans])
        phase = phase + jnp.where(fresh, 1, 0)
        for i, (_, _, first, _) in enumerate(spans):
            @pl.when(step == first)
            def _():
                left_copy(i).wait()
                if 0 < i < len(spans) - 1:
                    left_copy(i + 1).start()

        pltpu.make_async_copy(rights.at[slot], rights.at[slot], r_sem.at[slot]).wait()

        @pl.when(step >= 2)
        def _():
            wait_out(slot)

        units, halves = lefts.shape[1], lefts.shape[2]
        a_ref, b_ref = lefts.at[lax.rem(phase, 2)], rights.at[slot]
        a = jnp.concatenate([a_ref[k, t] for k in range(units) for t in range(halves)], 1)
        b = jnp.concatenate([jnp.concatenate([b_ref[k, j] for j in range(per)], 1) for k in range(units)], 0)
        tiles[slot] = mm(a, b)
        out_copy(step)
        return phase

    lax.fori_loop(0, steps, body, jnp.int32(-1))
    wait_out(0)
    wait_out(1)


def weight_grads(lefts, rights):
    units, halves, _, _ = lefts[0].shape
    height = rights[0].shape[2]
    hbm = pl.BlockSpec(memory_space=pl.ANY)
    dma = pltpu.SemaphoreType.DMA
    num = len(lefts)
    flops = sum(2 * units * height * a.shape[2] * b.shape[1] * LANE for a, b in zip(lefts, rights))

    def kernel(*refs):
        weight_kernel(refs[:num], refs[num : 2 * num], refs[2 * num : 3 * num], *refs[3 * num :])

    return pl.pallas_call(
        kernel,
        out_shape=[jax.ShapeDtypeStruct((a.shape[2], b.shape[1] * LANE), F32) for a, b in zip(lefts, rights)],
        in_specs=[hbm] * (2 * num),
        out_specs=[hbm] * num,
        scratch_shapes=[
            pltpu.VMEM((2, units, halves, TILE_M, LANE), BF16), pltpu.VMEM((2, units, TILE_N // LANE, height, LANE), BF16),
            pltpu.VMEM((2, TILE_M, TILE_N), F32), dma((2,)), dma((2,)), dma((2,))],
        compiler_params=pltpu.CompilerParams(vmem_limit_bytes=48 * 1024 * 1024),
        cost_estimate=pl.CostEstimate(flops=flops, bytes_accessed=200_000_000, transcendentals=0),
        name="weight_grads",
    )(*lefts, *rights)


def solution(mesh):
    num_stages = mesh.shape["stage"]

    def stage_program(embeds, targets, w_qkv, w_out, w_up, w_down):
        num_micro, batch_size, seq_len, model_dim = embeds.shape
        num_heads, head_dim = w_out.shape[1], w_out.shape[2]
        flat = (num_micro * batch_size, seq_len, model_dim)
        res = run_pipeline(
            "stage", num_stages, embeds.reshape(flat), targets.reshape(flat),
            w_qkv[0], w_out[0].reshape(num_heads * head_dim, model_dim), w_up[0], w_down[0], head_dim)
        u_t, ctx_t, z_t, gl_t, dqkv, dh, dpre, g, dx = res[:9]
        loss = res[-1]
        is_first = lax.axis_index("stage") == 0
        is_last = lax.axis_index("stage") == num_stages - 1
        dx = lax.psum(jnp.where(is_first, dx, jnp.zeros_like(dx)), "stage")
        total = lax.psum(jnp.where(is_last, jnp.sum(loss), 0.0), "stage").reshape(1)
        d_qkv, d_out, d_up, d_down = weight_grads((u_t, ctx_t, z_t, gl_t), (dqkv, dh, dpre, g))
        d_embeds = dx.transpose(0, 2, 1, 3).reshape(embeds.shape)
        return total, d_qkv[None], d_out.reshape(w_out.shape), d_up[None], d_down[None], d_embeds

    act_spec = P("rep", None, None, None)
    w3_spec = P("stage", None, None)
    g3_spec = P(("rep", "stage"), None, None)
    in_specs = (act_spec, act_spec, w3_spec, P("stage", None, None, None), w3_spec, w3_spec)
    out_specs = (P("rep"), g3_spec, P(("rep", "stage"), None, None, None), g3_spec, g3_spec, act_spec)
    return jax.shard_map(stage_program, mesh=mesh, in_specs=in_specs, out_specs=out_specs, check_vma=False)
```

time: 892 us -> 735 us (0.82); the launches traced: 876 us -> 734 us
  matrix products: 137 us -> 0 us
  Pallas kernels: 694 us -> 674 us
  local copies, waits for them, and re-layouts: 8.75 us -> 23.6 us
    dot_general x4 -> x0, matrix products: 137 us -> none  [stage_program(): jnp.einsum('usd,use->de', a, b, preferred_element_type=F32)]
    pallas_call x1, Pallas kernels: 694 us -> 559 us  [run_pipeline(): pl.pallas_call(functools.partial(pipeline_kernel, axis, stages, units, he...]
    pallas_call x0 -> x1, Pallas kernels: none -> 114 us  [weight_grads(): pl.pallas_call(kernel, out_shape=[jax.ShapeDtypeStruct((a.shape[2], b.sha...]
    transpose x0 -> x1, local copies, waits for them, and re-layouts: none -> 12.3 us  [stage_program(): d_embeds = dx.transpose(0, 2, 1, 3).reshape(embeds.shape)]
  transfers between devices with their start and end apart: 1 -> 1, of which waited for: 0 -> 0; matrix products, arithmetic and copies ran while one was open for 16% -> 0% of each run, Pallas kernels for 0% -> 16%
where the time goes in v2:
time: 735 us; the launch traced here: 734 us
  Pallas kernels  674 us (92%)
  local copies, waits for them, and re-layouts  23.6 us (3%)
  between operations  14.8 us (2%)
  blocking collectives  13.6 us (2%)
  other arithmetic  7.93 us (1%)
    pallas_call x1, Pallas kernels, run_pipeline(): pl.pallas_call(functools.partial(pipeline_kernel, axis, stages, units, he...  559 us
    pallas_call x1, Pallas kernels, weight_grads(): pl.pallas_call(kernel, out_shape=[jax.ShapeDtypeStruct((a.shape[2], b.sha...  114 us
  transfers between devices with their start and end apart: 1, of which 0 were waited for; matrix products, arithmetic and copies ran while one was open for 0% of the time, Pallas kernels for 16%

profile of v2, /device:TPU:112, one launch (start us, length us, event | category | flops | bytes accessed | tf_op | source)
XLA Modules:
  0.0 733.9 jit_solution(17165129694526987407)
XLA Ops:
  7.2 0.1 all-reduce.2.cloned.1.call-start
  7.3 559.4 %pipeline.1 = (bf16[16,2,1024,128]{3,2,1,0:T(8,128)(2,1)}, bf16[16,2,1024,128]{3,2,1,0:T(8,128)(2,1)}, bf16[16,2,1024,128]{3,2,1,0:T(8,128)(2,1)}, bf16[16,2,409...) custom-call(bf16[16,256,1024]{2,1,0:T(8,128)(2,1)} %bitcast.15, ...), custom_call_target="tpu_custom_call" | custom-call | tf_op jit(solution)/shard_map/pipeline/pallas_call | solution.py:541
  566.7 7.3 select_bitcast_fusion
  574.0 12.3 %copy.12 = bf16[16,256,8,128]{1,3,2,0:T(8,128)(2,1)} copy(bf16[16,256,8,128]{3,1,2,0:T(8,128)(2,1)} %select_bitcast_fusion) | data formatting | bytes 16777216 | tf_op jit(solution)/shard_map/transpose | solution.py:681
  586.3 0.1 all-reduce.2.cloned.1.call-update
  586.4 0.0 copy-start
  586.4 114.4 %weight_grads.1 = (f32[1024,3072]{1,0:T(8,128)}, f32[1024,1024]{1,0:T(8,128)}, f32[1024,4096]{1,0:T(8,128)}, f32[4096,1024]{1,0:T(8,128)}) custom-call(bf16[16,2,1024,128]{3,2,1,0:T(8,128)(2,1)} %get-tuple-element.21.refs_0_, bf16[16,2,1024,128]{3,2,1,0:T(8,128)(2,1)} %get-tuple-element.22.refs_1_, bf16[16,2,1024,128]{3,2,1,0:T(8,128)(2,1)} %get-tuple-element.23.refs_2_, ...), custom_call_target="tpu_custom_call" | custom-call | flops 103079215104 | bytes 200000000 | tf_op jit(solution)/shard_map/weight_grads/pallas_call | solution.py:650
  700.8 0.0 copy-done
  700.8 0.6 reduce_sum.9
  702.1 13.6 %psum.14 = f32[1]{0:T(128)} all-reduce(f32[1]{0:T(128)} %bitcast.6), channel_id=1, replica_groups=mesh['rep'=2,'stage'=8] {'stage'}, use_global_device_ids=true, to_apply=%region_1.2 | all-reduce | flops 1 | bytes 8 | tf_op jit(solution)/shard_map/psum | solution.py:679
  715.7 0.0 all-reduce.2.cloned.1.call-done
  715.7 11.4 %copy.13 = bf16[8,2,256,1024]{3,2,1,0:T(8,128)(2,1)} copy(bf16[8,2,256,1024]{2,3,1,0:T(8,128)(2,1)} %all-reduce.2.cloned.1.call-done) | data formatting | bytes 16777216
Async XLA Ops:
  7.2 708.5 %all-reduce.2.cloned.1.call-start = ((), (), s32[]{:S(2)}) async-start(), calls=%async_computation | async-start | bytes 16777216 | tf_op jit(solution)/shard_map/psum | solution.py:678
  586.4 114.5 %copy-start = (f32[8,128]{1,0:T(8,128)S(1)}, f32[8,128]{1,0:T(8,128)}, u32[]{:S(2)}) copy-start(f32[8,128]{1,0:T(8,128)} %get-tuple-element.20) | copy-start | bytes 12292
Sparse Core Ops, SparseCore 0:
  586.5 95.9 all-reduce.1

commit v3 on v2

v3 whole, which is shorter than its diff:
```python
import functools

import jax
import jax.numpy as jnp
from jax import lax
from jax.experimental import pallas as pl
from jax.experimental.pallas import tpu as pltpu
from jax.sharding import PartitionSpec as P


F32, BF16 = jnp.float32, jnp.bfloat16
MESH = pl.DeviceIdType.MESH
NORM_EPS = 1e-6
NEG_BIG = -1e30
GELU_SCALE, GELU_CUBE = 0.7978845608028654, 0.044715
LANE = 128
NORM_ROWS = 32
RING = 3
TILE_M, TILE_N = 1024, 512
GROUP = 6
SPLIT_UNITS = 5
TILES_BETWEEN, TILES_AFTER = 4, 8
VMEM_BYTES = 67043328


def mm(lhs, rhs):
    return jnp.dot(lhs, rhs, preferred_element_type=F32)


def mm_rt(lhs, rhs):
    return lax.dot_general(lhs, rhs, (((1,), (1,)), ((), ())), preferred_element_type=F32)


def mm_lt(lhs, rhs):
    return lax.dot_general(lhs, rhs, (((0,), (0,)), ((), ())), preferred_element_type=F32)


def cols(ref, lo, hi):
    return jnp.concatenate([ref[j] for j in range(lo, hi)], 1)


def rows_of(ref, lo, hi):
    return jnp.concatenate([ref[j, lo:hi, :] for j in range(ref.shape[0])], 1)


def pieces(vals):
    return [vals[:, LANE * j : LANE * j + LANE] for j in range(vals.shape[1] // LANE)]


def put(ref, lo, vals):
    for j, piece in enumerate(pieces(vals)):
        ref[lo + j] = piece


def accumulate(ref, vals, first):
    for j, piece in enumerate(pieces(vals)):
        ref[j] = piece if first else ref[j] + piece


def row_scale(sums, width):
    return jnp.sum(sums, axis=-1, keepdims=True) * (1.0 / width)


def norm_into(dst, load, starts):
    blocks = dst.shape[0]
    for r in starts:
        vals = [load(j, r) for j in range(blocks)]
        total = sum(v * v for v in vals)
        scale = lax.rsqrt(row_scale(total, blocks * LANE) + NORM_EPS)
        for j, v in enumerate(vals):
            dst[j, r : r + NORM_ROWS, :] = (v * scale).astype(BF16)


def norm_vjp_into(dst, base, load, d_load):
    blocks, height = dst.shape[0], dst.shape[1]
    width = blocks * LANE
    for r in range(0, height, NORM_ROWS):
        vals = [load(j, r) for j in range(blocks)]
        grads = [d_load(j, r) for j in range(blocks)]
        scale = lax.rsqrt(row_scale(sum(v * v for v in vals), width) + NORM_EPS)
        pull = scale * scale * scale * row_scale(sum(v * d for v, d in zip(vals, grads)), width)
        for j in range(blocks):
            dst[j, r : r + NORM_ROWS, :] = (base(j, r) + (grads[j] * scale - vals[j] * pull)).astype(BF16)


def reader(ref):
    return lambda j, r: ref[j, r : r + NORM_ROWS, :].astype(F32)


def rounded(ref):
    return lambda j, r: ref[j, r : r + NORM_ROWS, :].astype(BF16).astype(F32)


def gelu(x):
    t = jnp.tanh(x * (GELU_SCALE + (GELU_SCALE * GELU_CUBE) * (x * x)))
    return (0.5 * x) * (1.0 + t)


def gelu_grad(x):
    x_sq = x * x
    t = jnp.tanh(x * (GELU_SCALE + (GELU_SCALE * GELU_CUBE) * x_sq))
    up = 1.0 + t
    return 0.5 * (up + (((1.0 - t) * up) * x) * (GELU_SCALE + (3 * GELU_SCALE * GELU_CUBE) * x_sq))


def head_half(vals, which):
    lane = lax.broadcasted_iota(jnp.int32, (1, LANE), 1)
    return jnp.where((lane < LANE // 2) if which == 0 else (lane >= LANE // 2), vals, jnp.zeros_like(vals))


def split_heads(vals):
    return [head_half(vals, 0), head_half(vals, 1)]


def pair_scores(keys, queries, halves=(0, 1)):
    return [mm_rt(keys[: LANE * (t + 1)], queries[LANE * t : LANE * (t + 1)]) for t in halves]


def column_softmax(scores):
    e = jnp.exp(scores - jnp.max(scores, axis=0, keepdims=True))
    return e * (1.0 / jnp.sum(e, axis=0, keepdims=True))


def probs(scores, causal, scale, halves=(0, 1)):
    parts = []
    for t, s in zip(halves, scores):
        s = (s * scale).astype(BF16).astype(F32)
        below = jnp.where(causal, s[LANE * t :], NEG_BIG)
        parts.append(column_softmax(jnp.concatenate([s[: LANE * t], below], 0) if t else below))
    return parts


def causal_mask():
    return lax.broadcasted_iota(jnp.int32, (LANE, LANE), 0) <= lax.broadcasted_iota(jnp.int32, (LANE, LANE), 1)


def skip():
    pass


def layer_forward(halves, x, w_qkv, w_out, w_up, w_down, u, qkv, ctx_t, hid, pre, gl, out, acc, u_t, z_t, gl_t, scale, marks):
    blocks = x.shape[0]
    ff_blocks = w_up.shape[0]
    quads = blocks // 2
    half = LANE // 2
    causal = causal_mask()
    rows = slice(LANE * halves[0], LANE * (halves[-1] + 1))
    starts = range(rows.start, rows.stop, NORM_ROWS)
    norm_into(u, reader(x), starts)

    def lhs(ref, lo, hi):
        return jnp.concatenate([ref[j, rows, :] for j in range(lo, hi)], 1)

    def store(ref, lo, vals):
        for j, piece in enumerate(pieces(vals)):
            ref[lo + j, rows, :] = piece

    def gather(vals, first):
        for j, piece in enumerate(pieces(vals)):
            acc[j, rows, :] = piece if first else acc[j, rows, :] + piece

    def flip(dsts, src, lo, hi):
        per = dsts[0].shape[1] // LANE
        for j in range(lo, hi):
            at = slice(LANE * (j % per), LANE * (j % per) + LANE)
            for t, piece in zip(halves, pieces(src[j, rows, :].T)):
                dsts[j // per][t, at, :] = piece

    def project(i):
        for w in range(3):
            lo = w * blocks + 2 * i
            store(qkv, lo, mm(lhs(u, 0, blocks), cols(w_qkv, lo, lo + 2)).astype(BF16))

    def out_part(lo, hi):
        return mm_lt(jnp.concatenate([ctx_t[t, lo:hi, :] for t in halves], 1), rows_of(w_out, lo, hi))

    project(0)
    flip([u_t], u, 0, blocks)
    for i in range(quads):
        pairs = (2 * i, 2 * i + 1)
        scores = [pair_scores(k, qkv[p], halves) for p in pairs for k in split_heads(qkv[blocks + p])]
        if i < quads - 1:
            project(i + 1)
        else:
            marks.get("qkv", skip)()
            gather(out_part(0, 2 * LANE * i), True)
        a = [probs(s, causal, scale, halves) for s in scores]
        for j, p in enumerate(pairs):
            v_t = qkv[2 * blocks + p].T
            for h in range(2):
                at = slice(LANE * p + half * h, LANE * p + half * h + half)
                v_head = v_t[half * h : half * h + half]
                for t, a_part in zip(halves, a[2 * j + h]):
                    ctx_t[t, at, :] = mm(v_head[:, : LANE * (t + 1)], a_part.astype(BF16)).astype(BF16)
    gather(out_part(2 * LANE * (quads - 1), blocks * LANE), False)
    marks.get("ctx", skip)()
    for r in starts:
        for j in range(blocks):
            at = slice(r, r + NORM_ROWS)
            hid[j, at, :] = (x[j, at, :].astype(F32) + acc[j, at, :]).astype(BF16)
    norm_into(u, reader(hid), starts)
    step = 4
    up = lambda c: mm(lhs(u, 0, blocks), cols(w_up, c, c + step)).astype(BF16)
    cur = up(0)
    flip([z_t], u, 0, blocks)
    for c in range(0, ff_blocks, step):
        nxt = up(c + step) if c + step < ff_blocks else None
        for j, piece in enumerate(pieces(cur)):
            pre[c + j, rows, :] = piece
            gl[c + j, rows, :] = gelu(piece.astype(F32)).astype(BF16)
        flip(gl_t, gl, c, c + step)
        cur = nxt
    marks.get("ff", skip)()
    for j, piece in enumerate(pieces(mm(lhs(gl, 0, ff_blocks), cols(w_down, 0, blocks)))):
        out[j, rows, :] = (hid[j, rows, :].astype(F32) + piece).astype(BF16)


def layer_backward(g, x, hid, qkv, pre, w_qkv, w_out, w_up, w_down, d_qkv, d_ctx, d_hid, d_pre, out, acc, scale, marks):
    blocks = x.shape[0]
    ff_blocks = w_up.shape[0]
    quads = blocks // 2
    half = LANE // 2
    causal = causal_mask()
    step = 4
    down = lambda c: mm_rt(cols(g, 0, blocks), rows_of(w_down, LANE * c, LANE * (c + step))).astype(BF16)
    cur = down(0)
    for c in range(0, ff_blocks, step):
        nxt = down(c + step) if c + step < ff_blocks else None
        for j, piece in enumerate(pieces(cur)):
            d_pre[c + j] = (piece.astype(F32) * gelu_grad(pre[c + j].astype(F32))).astype(BF16)
        accumulate(acc, mm_rt(cols(d_pre, c, c + step), cols(w_up, c, c + step)), c == 0)
        cur = nxt
    norm_vjp_into(d_hid, reader(g), reader(hid), rounded(acc))
    marks["ff"]()

    def ctx_part(i):
        put(d_ctx, 2 * i, mm_rt(cols(d_hid, 0, blocks), rows_of(w_out, 2 * LANE * i, 2 * LANE * (i + 1))).astype(BF16))

    def qkv_part(i):
        take = lambda ref: jnp.concatenate([ref[w * blocks + 2 * i + t] for w in range(3) for t in range(2)], 1)
        accumulate(acc, mm_rt(take(d_qkv), take(w_qkv)), i == 0)

    ctx_part(0)
    for i in range(quads):
        pairs = (2 * i, 2 * i + 1)
        scores = [pair_scores(k, qkv[p]) for p in pairs for k in split_heads(qkv[blocks + p])]
        d_probs = [pair_scores(v, d_ctx[p]) for p in pairs for v in split_heads(qkv[2 * blocks + p])]
        if i < quads - 1:
            ctx_part(i + 1)
        if i > 0:
            qkv_part(i - 1)
        a, ds = [], []
        for s, dp in zip(scores, d_probs):
            a_pair = probs(s, causal, scale)
            dp = [d.astype(BF16).astype(F32) for d in dp]
            ds.append([(p * (d - jnp.sum(p * d, axis=0, keepdims=True))).astype(BF16) for p, d in zip(a_pair, dp)])
            a.append([p.astype(BF16) for p in a_pair])
        for j, p in enumerate(pairs):
            n = LANE

            def weigh(first, second, vals):
                top = mm(
                    jnp.concatenate([first[0], first[1][:n], second[0], second[1][:n]], 1), jnp.concatenate(vals, 0))
                low = mm(
                    jnp.concatenate([first[1][n:], second[1][n:]], 1), jnp.concatenate([vals[0][n:], vals[1][n:]], 0))
                return jnp.concatenate([top, low], 0)

            heads = (2 * j, 2 * j + 1)
            d_qkv[2 * blocks + p] = weigh(*(a[h] for h in heads), split_heads(d_ctx[p])).astype(BF16)
            d_qkv[blocks + p] = (weigh(*(ds[h] for h in heads), split_heads(qkv[p])) * scale).astype(BF16)
            k_t = qkv[blocks + p].T
            dq_t = []
            for h in range(2):
                k_head = k_t[half * h : half * h + half]
                d0, d1 = ds[heads[h]]
                dq_t.append(jnp.concatenate([mm(k_head[:, :n], d0), mm(k_head, d1)], 1) * scale)
            d_qkv[p] = jnp.concatenate(dq_t, 0).astype(BF16).T
    qkv_part(quads - 1)
    marks["qkv"]()
    norm_vjp_into(out, reader(d_hid), reader(x), rounded(acc))


class WeightTiles:
    def __init__(self, left_refs, right_refs, acc_refs, out_refs, lefts, rights, tiles, l_sem, r_sem, a_sem, o_sem, first_unit, bare):
        self.left_refs, self.right_refs, self.acc_refs, self.out_refs = left_refs, right_refs, acc_refs, out_refs
        self.lefts, self.rights, self.tiles = lefts, rights, tiles
        self.l_sem, self.r_sem, self.a_sem, self.o_sem = l_sem, r_sem, a_sem, o_sem
        self.first_unit, self.bare = first_unit, bare
        self.units, self.halves = lefts.shape[1], lefts.shape[2]
        self.slots = tiles.shape[0]
        self.spans, self.steps = [], 0
        for w, (a, b) in enumerate(zip(left_refs, right_refs)):
            count = b.shape[1] * LANE // TILE_N
            for m in range(a.shape[2] // TILE_M):
                self.spans.append((w, m, self.steps, count))
                self.steps += count

    def group_units(self, group):
        return pl.ds(self.first_unit + group * self.units, self.units)

    def left_copy(self, k, group):
        w, m = self.spans[k][:2]
        src = self.left_refs[w].at[self.group_units(group), :, pl.ds(m * TILE_M, TILE_M), :]
        return pltpu.make_async_copy(src, self.lefts.at[k % 2], self.l_sem.at[k % 2])

    def each_span(self, j, fn):
        for w, m, first, count in self.spans:
            @pl.when((j >= first) & (j < first + count))
            def _():
                fn(w, m, j - first)

    def window(self, refs, w, m, n):
        return refs[w].at[pl.ds(m * TILE_M, TILE_M), pl.ds(pl.multiple_of(n * TILE_N, TILE_N), TILE_N)]

    def load(self, i):
        group, j = i // self.steps, lax.rem(i, self.steps)
        slot, tile = lax.rem(i, 2), lax.rem(i, self.slots)
        per = TILE_N // LANE

        @pl.when(i >= self.slots)
        def _():
            self.wait_store(tile)

        def start(w, m, n):
            src = self.right_refs[w].at[self.group_units(group), pl.ds(n * per, per)]
            pltpu.make_async_copy(src, self.rights.at[slot], self.r_sem.at[slot]).start()

            @pl.when(group >= self.bare)
            def _():
                pltpu.make_async_copy(
                    self.window(self.acc_refs, w, m, n), self.tiles.at[tile], self.a_sem.at[tile]).start()

        self.each_span(j, start)

    def wait_store(self, tile):
        pltpu.make_async_copy(self.tiles.at[tile], self.tiles.at[tile], self.o_sem.at[tile]).wait()

    def step(self, i):
        group, j = i // self.steps, lax.rem(i, self.steps)
        slot, tile = lax.rem(i, 2), lax.rem(i, self.slots)

        @pl.when(j == 0)
        def _():
            self.left_copy(0, group).start()
            self.load(i)
            self.left_copy(1, group).start()

        @pl.when(j + 1 < self.steps)
        def _():
            self.load(i + 1)

        chunk = -1
        for k, (_, _, first, _) in enumerate(self.spans):
            chunk = chunk + jnp.where(j >= first, 1, 0)

            @pl.when(j == first)
            def _():
                self.left_copy(k, group).wait()
                if 0 < k < len(self.spans) - 1:
                    self.left_copy(k + 1, group).start()

        pltpu.make_async_copy(self.rights.at[slot], self.rights.at[slot], self.r_sem.at[slot]).wait()

        @pl.when(group >= self.bare)
        def _():
            pltpu.make_async_copy(self.tiles.at[tile], self.tiles.at[tile], self.a_sem.at[tile]).wait()

        a_ref, b_ref = self.lefts.at[lax.rem(chunk, 2)], self.rights.at[slot]
        a = jnp.concatenate([a_ref[k, t] for k in range(self.units) for t in range(self.halves)], 1)
        b = jnp.concatenate([cols(b_ref.at[k], 0, TILE_N // LANE) for k in range(self.units)], 0)
        fresh = mm(a, b)
        if self.bare == 0:
            self.tiles[tile] = self.tiles[tile] + fresh
        else:
            self.tiles[tile] = jnp.where(group >= self.bare, self.tiles[tile], 0.0) + fresh

        def store(w, m, n):
            pltpu.make_async_copy(self.tiles.at[tile], self.window(self.out_refs, w, m, n), self.o_sem.at[tile]).start()

        self.each_span(j, store)


def pipeline_kernel(
    axis, stages, units, scale, inv_count,
    embeds, targets, w_qkv_h, w_out_h, w_up_h, w_down_h,
    ut_all, ctx_all, zt_all, glt_all, dqkv_all, dh_all, dpre_all, g_all, dx_all,
    gw_qkv, gw_out, gw_up, gw_down, qkv_all, h_all, pre_all, x_all, loss,
    w_qkv, w_out, w_up, w_down, act, grad, out, d_in,
    tmp_act, tmp_mid, tmp_ff, qkv, hid, pre, acc, dqkv, lefts, rights, tiles,
    w_sem, emb_sem, tgt_sem, f_send, f_recv, f_free, b_send, b_recv, b_free, f_save, b_save, b_load,
    x_send, x_recv, l_send, l_recv, wl_sem, wr_sem, wa_sem, wo_sem,
):
    stage = lax.axis_index(axis)
    last = stages - 1
    blocks, height = act.shape[1], act.shape[2]
    halves = range(height // LANE)
    right, left = lax.rem(stage + 1, stages), lax.rem(stage + last, stages)
    u = dctx = tmp_act
    target = dh = tmp_mid
    gl = dpre = tmp_ff
    chunks = w_down.shape[1] // TILE_M
    gl_t = [lefts.at[0, k] for k in range(chunks)]
    u_t, z_t, ctx_t = lefts.at[0, chunks], lefts.at[0, chunks + 1], lefts.at[1, 0]
    gw = (gw_qkv, gw_out, gw_up, gw_down)
    work = WeightTiles(
        (ut_all, ctx_all, zt_all, glt_all), (dqkv_all, dh_all, dpre_all, g_all), gw, gw, lefts, rights, tiles,
        wl_sem, wr_sem, wa_sem, wo_sem, 0, 1)
    groups = units // GROUP
    total_tiles = groups * work.steps
    barrier = pltpu.get_barrier_semaphore()
    for ahead in range(1, stages):
        pl.semaphore_signal(
            barrier, inc=1, device_id={axis: lax.rem(stage + ahead, stages)}, device_id_type=MESH)

    def load_columns(src, dst, sem):
        def start(j, carry):
            pltpu.make_async_copy(src.at[:, pl.ds(pl.multiple_of(j * LANE, LANE), LANE)], dst.at[j], sem).start()
            return carry

        lax.fori_loop(0, dst.shape[0], start, 0)

    def wait_whole(ref, sem):
        pltpu.make_async_copy(ref, ref, sem).wait()

    def embed_slot(unit):
        return act.at[lax.rem(unit, RING)], emb_sem.at[lax.rem(unit, RING)]

    def embed_start(unit):
        load_columns(embeds.at[unit], *embed_slot(unit))

    weights = ((w_qkv_h, w_qkv), (w_out_h, w_out), (w_up_h, w_up), (w_down_h, w_down))

    @pl.when(stage == 0)
    def _():
        embed_start(0)

    for i, (src, dst) in enumerate(weights):
        load_columns(src, dst, w_sem.at[i])

    @pl.when(stage == 0)
    def _():
        embed_start(1)

    loss[...] = jnp.zeros_like(loss)
    pl.semaphore_wait(barrier, last)

    def f_copy(unit, half):
        slot, ring = lax.rem(unit, 2), lax.rem(unit, RING)
        at = pl.ds(half * LANE, LANE)
        return pltpu.make_async_remote_copy(
            src_ref=out.at[slot, :, at, :], dst_ref=act.at[ring, :, at, :], send_sem=f_send.at[slot, half],
            recv_sem=f_recv.at[ring, half], device_id={axis: right}, device_id_type=MESH)

    def b_copy(unit):
        slot, ring = lax.rem(unit, 2), lax.rem(unit, RING)
        return pltpu.make_async_remote_copy(
            src_ref=d_in.at[slot], dst_ref=grad.at[ring], send_sem=b_send.at[slot], recv_sem=b_recv.at[ring],
            device_id={axis: left}, device_id_type=MESH)

    even = lax.rem(stage, 2) == 0
    chain = even & ((stage == 0) | (stage + 2 < stages - 2))
    branches = ((even, right), (chain, lax.rem(stage + 2, stages)), (stage == 0, stages - 2))

    def x_copies(unit, src):
        slot = lax.rem(unit, 2)
        return [
            (cond, pltpu.make_async_remote_copy(
                src_ref=src, dst_ref=dx_all.at[unit], send_sem=x_send.at[slot, k], recv_sem=x_recv.at[unit],
                device_id={axis: dest}, device_id_type=MESH))
            for k, (cond, dest) in enumerate(branches)]

    def x_start(unit, src):
        for cond, copy in x_copies(unit, src):
            @pl.when(cond)
            def _():
                copy.start()

    def x_wait_send(unit):
        for cond, copy in x_copies(unit, dx_all.at[unit]):
            @pl.when(cond)
            def _():
                copy.wait_send()

    def x_wait_recv(unit):
        x_copies(unit, dx_all.at[unit])[0][1].wait_recv()

    def dx_copy(unit):
        slot = lax.rem(unit, 2)
        return pltpu.make_async_copy(d_in.at[slot], dx_all.at[unit], b_send.at[slot])

    def loss_copy(k):
        return pltpu.make_async_remote_copy(
            src_ref=loss, dst_ref=loss, send_sem=l_send.at[k], recv_sem=l_recv, device_id={axis: k}, device_id_type=MESH)

    def f_saves(unit):
        pairs = [
            (act.at[lax.rem(unit, RING)], x_all.at[unit]), (u_t, ut_all.at[unit]), (qkv.at[0], qkv_all.at[unit]),
            (ctx_t, ctx_all.at[unit]), (hid.at[0], h_all.at[unit]), (z_t, zt_all.at[unit]), (pre.at[0], pre_all.at[unit])]
        pairs += [(ref, glt_all.at[unit, :, pl.ds(k * TILE_M, TILE_M), :]) for k, ref in enumerate(gl_t)]
        return [pltpu.make_async_copy(src, dst, f_save.at[i]) for i, (src, dst) in enumerate(pairs)]

    def b_saves(unit):
        pairs = ((grad.at[lax.rem(unit, RING)], g_all), (dqkv, dqkv_all), (dpre, dpre_all), (dh, dh_all))
        return [pltpu.make_async_copy(src, dst.at[unit], b_save.at[i]) for i, (src, dst) in enumerate(pairs)]

    def b_loads(unit):
        pairs = (
            (pre_all, pre.at[1]), (h_all, hid.at[1]), (qkv_all, qkv.at[1]), (x_all, act.at[RING + lax.rem(unit, 2)]))
        return [pltpu.make_async_copy(src.at[unit], dst, b_load.at[i]) for i, (src, dst) in enumerate(pairs)]

    def wait_late_saves(unit):
        for copy in b_saves(unit)[:2]:
            copy.wait()

    work_start = jnp.maximum(GROUP - 1 + 2 * last - stage, units + stage)
    b_end = units - 1 + 2 * last - stage

    def tiles_by(t):
        between = jnp.maximum(jnp.minimum(t, b_end) - work_start + 1, 0)
        return jnp.minimum(TILES_BETWEEN * between + TILES_AFTER * jnp.maximum(t - b_end, 0), total_tiles)

    def make_tiles(first, end):
        lax.fori_loop(first, end, lambda i, c: (work.step(i), c)[1], 0)

    def forward(unit):
        ring, slot = lax.rem(unit, RING), lax.rem(unit, 2)
        saves = f_saves(unit)

        @pl.when(stage == last)
        def _():
            load_columns(targets.at[unit], target, tgt_sem)

        @pl.when((stage == 0) & (unit + 2 < units))
        def _():
            embed_start(unit + 2)

        @pl.when((stage < last) & (unit >= 2))
        def _():
            for half in halves:
                f_copy(unit, half).wait_send()

        def run(part, marks):
            layer_forward(
                part, act.at[ring], w_qkv, w_out, w_up, w_down, u, qkv.at[0], ctx_t, hid.at[0], pre.at[0], gl,
                out.at[slot], acc, u_t, z_t, gl_t, scale, marks)

        def arrive(half):
            @pl.when((stage == 0) & (half == 0))
            def _():
                wait_whole(*embed_slot(unit))

            @pl.when(stage > 0)
            def _():
                f_copy(unit, half).wait_recv()

        def leave(half):
            @pl.when(stage < last)
            def _():
                f_copy(unit, half).start()

        def credit():
            @pl.when((stage < last) & (unit >= RING))
            def _():
                pl.semaphore_wait(f_free, 1)

        def weights_ready(*which):
            def wait():
                @pl.when(unit == 0)
                def _():
                    for w in which:
                        wait_whole(weights[w][1], w_sem.at[w])

            return wait

        @pl.when(unit < SPLIT_UNITS)
        def _():
            arrive(0)
            weights_ready(0)()
            run((0,), {"qkv": weights_ready(1), "ctx": weights_ready(2), "ff": weights_ready(3)})
            credit()
            leave(0)
            arrive(1)
            run((1,), {})
            leave(1)

        @pl.when(unit >= SPLIT_UNITS)
        def _():
            arrive(0)
            arrive(1)
            run((0, 1), {})
            credit()
            leave(0)
            leave(1)

        for copy in saves:
            copy.start()

        @pl.when(stage == last)
        def _():
            wait_whole(target, tgt_sem)
            part = jnp.zeros((8, LANE), F32)
            for j in range(blocks):
                err = out[slot, j].astype(F32) - target[j].astype(F32)
                grad[ring, j] = (err * inv_count).astype(BF16)
                part += jnp.sum((err * err).reshape(height // 8, 8, LANE), axis=0)
            loss[...] += part * (0.5 * inv_count)

        @pl.when((stage == last) & (unit == units - 1))
        def _():
            for k in range(stages - 1):
                loss_copy(k).start()

    def backward(unit, saved):
        ring, slot = lax.rem(unit, RING), lax.rem(unit, 2)
        src = jnp.where(stage == last, 0, 1)
        x_slot = jnp.where(stage == last, ring, RING + slot)
        saves = b_saves(unit)
        following = b_loads(unit + 1)
        more = (stage < last) & (unit + 1 < units)

        @pl.when(unit > 0)
        def _():
            @pl.when(jnp.logical_not(saved))
            def _():
                wait_late_saves(unit - 1)

            @pl.when((stage < last) & (unit - 1 < units - RING))
            def _():
                pl.semaphore_signal(b_free, inc=1, device_id={axis: right}, device_id_type=MESH)

        @pl.when(unit >= 2)
        def _():
            @pl.when(stage > 0)
            def _():
                b_copy(unit).wait_send()

            @pl.when(stage == 0)
            def _():
                dx_copy(unit).wait()
                x_wait_send(unit)

        @pl.when(stage < last)
        def _():
            b_copy(unit).wait_recv()
            for copy in b_loads(unit):
                copy.wait()

        saves[0].start()

        def ff_ready():
            saves[2].start()
            saves[3].start()

            @pl.when(more)
            def _():
                for i in (0, 1, 3):
                    following[i].start()

        def qkv_ready():
            saves[1].start()

            @pl.when(more)
            def _():
                following[2].start()

        layer_backward(
            grad.at[ring], act.at[x_slot], hid.at[src], qkv.at[src], pre.at[src], w_qkv, w_out, w_up, w_down,
            dqkv, dctx, dh, dpre, d_in.at[slot], acc, scale, {"ff": ff_ready, "qkv": qkv_ready})

        @pl.when((stage > 0) & (unit >= RING))
        def _():
            pl.semaphore_wait(b_free, 1)

        @pl.when(stage > 0)
        def _():
            b_copy(unit).start()

        @pl.when(stage == 0)
        def _():
            dx_copy(unit).start()
            x_start(unit, d_in.at[slot])

        saves[2].wait()
        saves[3].wait()

    def tick(t, carry):
        f_unit = t - stage
        b_unit = t - 2 * last + stage
        before, first, end = tiles_by(t - 2), tiles_by(t - 1), tiles_by(t)

        @pl.when((f_unit >= 1) & (f_unit <= units))
        def _():
            for copy in f_saves(f_unit - 1):
                copy.wait()

            @pl.when((stage > 0) & (f_unit - 1 < units - RING))
            def _():
                pl.semaphore_signal(f_free, inc=1, device_id={axis: left}, device_id_type=MESH)

        @pl.when((stage < last) & (b_unit == 0))
        def _():
            for copy in b_loads(0):
                copy.start()

        @pl.when((f_unit >= 0) & (f_unit < units))
        def _():
            forward(f_unit)

        @pl.when((b_unit >= 0) & (b_unit < units))
        def _():
            backward(b_unit, first > before)

            @pl.when(end > first)
            def _():
                wait_late_saves(b_unit)

        make_tiles(first, end)
        x_unit = t - 2 * last

        @pl.when(even & (stage > 0) & (x_unit >= 0))
        def _():
            x_wait_recv(x_unit)

            @pl.when(x_unit >= 2)
            def _():
                x_wait_send(x_unit)

            x_start(x_unit, dx_all.at[x_unit])

        return carry

    ticks = units + 2 * last
    lax.fori_loop(0, ticks, tick, 0)

    @pl.when(tiles_by(b_end) == tiles_by(b_end - 1))
    def _():
        wait_late_saves(units - 1)

    make_tiles(tiles_by(ticks - 1), total_tiles)

    for tile in range(work.slots):
        work.wait_store(tile)

    for unit in (units - 2, units - 1):
        @pl.when(stage < last)
        def _():
            for half in halves:
                f_copy(unit, half).wait_send()

        @pl.when(stage > 0)
        def _():
            b_copy(unit).wait_send()

        @pl.when(stage == 0)
        def _():
            dx_copy(unit).wait()

        x_wait_send(unit)

    @pl.when(jnp.logical_not(even))
    def _():
        lax.fori_loop(0, units, lambda unit, c: (x_wait_recv(unit), c)[1], 0)

    @pl.when(stage < last)
    def _():
        loss_copy(0).wait_recv()

    @pl.when(stage == last)
    def _():
        for k in range(stages - 1):
            loss_copy(k).wait_send()


def run_pipeline(axis, stages, embeds, targets, w_qkv, w_out, w_up, w_down, head_dim):
    units, height, width = embeds.shape
    n, ff = width // LANE, w_up.shape[1] // LANE
    halves = height // LANE
    saved = lambda *shape: jax.ShapeDtypeStruct((units,) + shape, BF16)
    rows_t = lambda k: saved(k, height, LANE)
    cols_t = lambda k: saved(halves, k, LANE)
    hbm = pl.BlockSpec(memory_space=pl.ANY)
    vm = lambda *shape: pltpu.VMEM(shape, BF16)
    rows = lambda *lead: vm(*lead, height, LANE)
    dma, regular = pltpu.SemaphoreType.DMA, pltpu.SemaphoreType.REGULAR
    outs = [
        cols_t(width), cols_t(width), cols_t(width), cols_t(ff * LANE), rows_t(3 * n), rows_t(n), rows_t(ff), rows_t(n), rows_t(n)]
    outs += [jax.ShapeDtypeStruct(w.shape, F32) for w in (w_qkv, w_out, w_up, w_down)]
    outs += [rows_t(3 * n), rows_t(n), rows_t(ff), rows_t(n), jax.ShapeDtypeStruct((8, LANE), F32)]
    return pl.pallas_call(
        functools.partial(pipeline_kernel, axis, stages, units, head_dim ** -0.5, 1.0 / (units * height * width)),
        out_shape=outs,
        in_specs=[hbm] * 6,
        out_specs=[hbm] * 17 + [pl.BlockSpec(memory_space=pltpu.VMEM)],
        scratch_shapes=[
            vm(3 * n, width, LANE), vm(n, width, LANE), vm(ff, width, LANE), vm(n, ff * LANE, LANE),
            rows(RING + 2, n), rows(RING, n), rows(2, n), rows(2, n),
            rows(n), rows(n), rows(ff), rows(2, 3 * n), rows(2, n), rows(2, ff), pltpu.VMEM((n, height, LANE), F32), rows(3 * n),
            vm(2, GROUP, halves, TILE_M, LANE), rows(2, GROUP, TILE_N // LANE), pltpu.VMEM((3, TILE_M, TILE_N), F32),
            dma((4,)), dma((RING,)), dma, dma((2, halves)), dma((RING, halves)), regular,
            dma((2,)), dma((RING,)), regular, dma((7 + ff * LANE // TILE_M,)), dma((4,)), dma((4,)),
            dma((2, 3)), dma((units,)), dma((stages - 1,)), dma, dma((2,)), dma((2,)), dma((3,)), dma((3,)),
        ],
        compiler_params=pltpu.CompilerParams(collective_id=0, has_side_effects=True, vmem_limit_bytes=VMEM_BYTES),
        name="pipeline",
    )(embeds, targets, w_qkv, w_out, w_up, w_down)


def finish_kernel(num, first_unit, *refs):
    left_refs, right_refs, acc_refs, dx, out_refs, d_embeds = (
        refs[:num], refs[num : 2 * num], refs[2 * num : 3 * num], refs[3 * num], refs[3 * num + 1 : 4 * num + 1], refs[4 * num + 1])
    lefts, rights, tiles, flat, l_sem, r_sem, a_sem, o_sem, in_sem, put_sem = refs[4 * num + 2 :]
    work = WeightTiles(
        left_refs, right_refs, acc_refs, out_refs, lefts, rights, tiles, l_sem, r_sem, a_sem, o_sem, first_unit, 0)
    units = dx.shape[0]

    def fetch(unit):
        slot = lax.rem(unit, 2)
        return pltpu.make_async_copy(dx.at[unit], flat.at[slot], in_sem.at[slot])

    def wait_put(slot):
        pltpu.make_async_copy(flat.at[slot], flat.at[slot], put_sem.at[slot]).wait()

    def relayout(i):
        @pl.when(i < units)
        def _():
            @pl.when(i >= 2)
            def _():
                wait_put(lax.rem(i, 2))

            fetch(i).start()

        @pl.when((i >= 1) & (i <= units))
        def _():
            unit, slot = i - 1, lax.rem(i - 1, 2)
            fetch(unit).wait()
            for j in range(dx.shape[1]):
                pltpu.make_async_copy(
                    flat.at[slot, j], d_embeds.at[unit, :, pl.ds(j * LANE, LANE)], put_sem.at[slot]).start()

    def body(i, carry):
        relayout(i)
        work.step(i)
        return carry

    lax.fori_loop(0, work.steps, body, 0)
    for i in range(work.steps, units + 1):
        relayout(i)
    for slot in range(2):
        wait_put(slot)
    for tile in range(work.slots):
        work.wait_store(tile)


def finish(lefts, rights, sums, dx):
    units, blocks, height, _ = dx.shape
    halves = height // LANE
    first_unit = units // GROUP * GROUP
    rest = units - first_unit
    num = len(lefts)
    hbm = pl.BlockSpec(memory_space=pl.ANY)
    dma = pltpu.SemaphoreType.DMA
    return pl.pallas_call(
        functools.partial(finish_kernel, num, first_unit),
        out_shape=[jax.ShapeDtypeStruct(s.shape, F32) for s in sums] + [jax.ShapeDtypeStruct((units, height, blocks * LANE), BF16)],
        in_specs=[hbm] * (3 * num + 1),
        out_specs=[hbm] * (num + 1),
        scratch_shapes=[
            pltpu.VMEM((2, rest, halves, TILE_M, LANE), BF16), pltpu.VMEM((2, rest, TILE_N // LANE, height, LANE), BF16),
            pltpu.VMEM((4, TILE_M, TILE_N), F32), pltpu.VMEM((2, blocks, height, LANE), BF16),
            dma((2,)), dma((2,)), dma((4,)), dma((4,)), dma((2,)), dma((2,))],
        compiler_params=pltpu.CompilerParams(vmem_limit_bytes=VMEM_BYTES),
        name="finish",
    )(*lefts, *rights, *sums, dx)


def solution(mesh):
    num_stages = mesh.shape["stage"]

    def stage_program(embeds, targets, w_qkv, w_out, w_up, w_down):
        num_micro, batch_size, seq_len, model_dim = embeds.shape
        num_heads, head_dim = w_out.shape[1], w_out.shape[2]
        flat = (num_micro * batch_size, seq_len, model_dim)
        res = run_pipeline(
            "stage", num_stages, embeds.reshape(flat), targets.reshape(flat),
            w_qkv[0], w_out[0].reshape(num_heads * head_dim, model_dim), w_up[0], w_down[0], head_dim)
        d_qkv, d_out, d_up, d_down, d_embeds = finish(res[:4], res[4:8], res[9:13], res[8])
        total = jnp.sum(res[-1]).reshape(1)
        return total, d_qkv[None], d_out.reshape(w_out.shape), d_up[None], d_down[None], d_embeds.reshape(embeds.shape)

    act_spec = P("rep", None, None, None)
    w3_spec = P("stage", None, None)
    g3_spec = P(("rep", "stage"), None, None)
    in_specs = (act_spec, act_spec, w3_spec, P("stage", None, None, None), w3_spec, w3_spec)
    out_specs = (P("rep"), g3_spec, P(("rep", "stage"), None, None, None), g3_spec, g3_spec, act_spec)
    return jax.shard_map(stage_program, mesh=mesh, in_specs=in_specs, out_specs=out_specs, check_vma=False)
```

time: 735 us -> 634 us (0.86)
  Pallas kernels: 674 us -> 632 us
  local copies, waits for them, and re-layouts: 23.6 us -> 0 us
  between operations: 14.8 us -> 0.64 us
  blocking collectives: 13.6 us -> 0 us
    pallas_call x1, Pallas kernels: 114 us -> 62.8 us  [finish(): pl.pallas_call(functools.partial(finish_kernel, num, first_unit), out_sha...]
    psum x1 -> x0, blocking collectives: 13.6 us -> none  [stage_program(): total = lax.psum(jnp.where(is_last, jnp.sum(loss), 0.0), 'stage').reshape(1)]
    transpose x1 -> x0, local copies, waits for them, and re-layouts: 12.3 us -> none  [stage_program(): d_embeds = dx.transpose(0, 2, 1, 3).reshape(embeds.shape)]
    unnamed x3 -> x0, local copies, waits for them, and re-layouts: 11.4 us -> none
    pallas_call x1, Pallas kernels: 559 us -> 569 us  [run_pipeline(): pl.pallas_call(functools.partial(pipeline_kernel, axis, stages, units, he...]
  transfers between devices with their start and end apart: 1 -> 0, of which waited for: 0 -> 0; matrix products, arithmetic and copies ran while one was open for 0% -> 0% of each run, Pallas kernels for 16% -> 0%
where the time goes in v3:
time: 634 us
  Pallas kernels  632 us (100%)
    pallas_call x1, Pallas kernels, run_pipeline(): pl.pallas_call(functools.partial(pipeline_kernel, axis, stages, units, he...  569 us
    pallas_call x1, Pallas kernels, finish(): pl.pallas_call(functools.partial(finish_kernel, num, first_unit), out_sha...  62.8 us

profile of v3, /device:TPU:112, one launch (start us, length us, event | category | flops | bytes accessed | tf_op | source)
XLA Modules:
  0.0 633.7 jit_solution(17690255415678460797)
XLA Ops:
  0.6 569.0 %pipeline.1 = (bf16[16,2,1024,128]{3,2,1,0:T(8,128)(2,1)}, bf16[16,2,1024,128]{3,2,1,0:T(8,128)(2,1)}, bf16[16,2,1024,128]{3,2,1,0:T(8,128)(2,1)}, bf16[16,2,409...) custom-call(bf16[16,256,1024]{2,1,0:T(8,128)(2,1)} %bitcast.12, ...), custom_call_target="tpu_custom_call" | custom-call | tf_op jit(solution)/shard_map/pipeline/pallas_call | solution.py:789
  569.6 1.3 reduce_sum.9
  570.9 62.8 %finish.1 = (f32[1024,3072]{1,0:T(8,128)}, f32[1024,1024]{1,0:T(8,128)}, f32[1024,4096]{1,0:T(8,128)}, f32[4096,1024]{1,0:T(8,128)}, bf16[16,256,1024]{2,1,0:T(8,128)(2,1)}) custom-call(bf16[16,2,1024,128]{3,2,1,0:T(8,128)(2,1)} %get-tuple-element.26.refs_0_, bf16[16,2,1024,128]{3,2,1,0:T(8,128)(2,1)} %get-tuple-element.27.refs_1_, ...), custom_call_target="tpu_custom_call" | custom-call | tf_op jit(solution)/shard_map/finish/pallas_call | solution.py:862

commit v4 on v3

--- a/solution.py
+++ b/solution.py
@@ -17,9 +17,9 @@
 NORM_ROWS = 32
 RING = 3
 TILE_M, TILE_N = 1024, 512
-GROUP = 6
+GROUP, GROUPS = 7, 1
 SPLIT_UNITS = 5
-TILES_BETWEEN, TILES_AFTER = 4, 8
+TILES_BETWEEN, TILES_AFTER = 3, 8
 VMEM_BYTES = 67043328
 
 
@@ -285,9 +285,10 @@
         self.left_refs, self.right_refs, self.acc_refs, self.out_refs = left_refs, right_refs, acc_refs, out_refs
         self.lefts, self.rights, self.tiles = lefts, rights, tiles
         self.l_sem, self.r_sem, self.a_sem, self.o_sem = l_sem, r_sem, a_sem, o_sem
-        self.first_unit, self.bare = first_unit, bare
+        self.first_unit = first_unit
         self.units, self.halves = lefts.shape[1], lefts.shape[2]
-        self.slots = tiles.shape[0]
+        self.slots, self.ahead = tiles.shape[0], rights.shape[0] - 1
+        self.sums = bare == 0
         self.spans, self.steps = [], 0
         for w, (a, b) in enumerate(zip(left_refs, right_refs)):
             count = b.shape[1] * LANE // TILE_N
@@ -314,19 +315,19 @@
 
     def load(self, i):
         group, j = i // self.steps, lax.rem(i, self.steps)
-        slot, tile = lax.rem(i, 2), lax.rem(i, self.slots)
+        slot, tile = lax.rem(i, self.ahead + 1), lax.rem(i, self.slots)
         per = TILE_N // LANE
 
         @pl.when(i >= self.slots)
         def _():
-            self.wait_store(tile)
+            if self.sums:
+                self.wait_store(tile)
 
         def start(w, m, n):
             src = self.right_refs[w].at[self.group_units(group), pl.ds(n * per, per)]
             pltpu.make_async_copy(src, self.rights.at[slot], self.r_sem.at[slot]).start()
 
-            @pl.when(group >= self.bare)
-            def _():
+            if self.sums:
                 pltpu.make_async_copy(
                     self.window(self.acc_refs, w, m, n), self.tiles.at[tile], self.a_sem.at[tile]).start()
 
@@ -337,17 +338,18 @@
 
     def step(self, i):
         group, j = i // self.steps, lax.rem(i, self.steps)
-        slot, tile = lax.rem(i, 2), lax.rem(i, self.slots)
+        slot, tile = lax.rem(i, self.ahead + 1), lax.rem(i, self.slots)
 
         @pl.when(j == 0)
         def _():
             self.left_copy(0, group).start()
-            self.load(i)
+            for d in range(self.ahead):
+                self.load(i + d)
             self.left_copy(1, group).start()
 
-        @pl.when(j + 1 < self.steps)
-        def _():
-            self.load(i + 1)
+        @pl.when(j + self.ahead < self.steps)
+        def _():
+            self.load(i + self.ahead)
 
         chunk = -1
         for k, (_, _, first, _) in enumerate(self.spans):
@@ -361,18 +363,18 @@
 
         pltpu.make_async_copy(self.rights.at[slot], self.rights.at[slot], self.r_sem.at[slot]).wait()
 
-        @pl.when(group >= self.bare)
-        def _():
+        if self.sums:
             pltpu.make_async_copy(self.tiles.at[tile], self.tiles.at[tile], self.a_sem.at[tile]).wait()
+        else:
+            @pl.when(i >= self.slots)
+            def _():
+                self.wait_store(tile)
 
         a_ref, b_ref = self.lefts.at[lax.rem(chunk, 2)], self.rights.at[slot]
         a = jnp.concatenate([a_ref[k, t] for k in range(self.units) for t in range(self.halves)], 1)
         b = jnp.concatenate([cols(b_ref.at[k], 0, TILE_N // LANE) for k in range(self.units)], 0)
         fresh = mm(a, b)
-        if self.bare == 0:
-            self.tiles[tile] = self.tiles[tile] + fresh
-        else:
-            self.tiles[tile] = jnp.where(group >= self.bare, self.tiles[tile], 0.0) + fresh
+        self.tiles[tile] = self.tiles[tile] + fresh if self.sums else fresh
 
         def store(w, m, n):
             pltpu.make_async_copy(self.tiles.at[tile], self.window(self.out_refs, w, m, n), self.o_sem.at[tile]).start()
@@ -405,8 +407,7 @@
     work = WeightTiles(
         (ut_all, ctx_all, zt_all, glt_all), (dqkv_all, dh_all, dpre_all, g_all), gw, gw, lefts, rights, tiles,
         wl_sem, wr_sem, wa_sem, wo_sem, 0, 1)
-    groups = units // GROUP
-    total_tiles = groups * work.steps
+    total_tiles = GROUPS * work.steps
     barrier = pltpu.get_barrier_semaphore()
     for ahead in range(1, stages):
         pl.semaphore_signal(
@@ -795,10 +796,10 @@
             vm(3 * n, width, LANE), vm(n, width, LANE), vm(ff, width, LANE), vm(n, ff * LANE, LANE),
             rows(RING + 2, n), rows(RING, n), rows(2, n), rows(2, n),
             rows(n), rows(n), rows(ff), rows(2, 3 * n), rows(2, n), rows(2, ff), pltpu.VMEM((n, height, LANE), F32), rows(3 * n),
-            vm(2, GROUP, halves, TILE_M, LANE), rows(2, GROUP, TILE_N // LANE), pltpu.VMEM((3, TILE_M, TILE_N), F32),
+            vm(2, GROUP, halves, TILE_M, LANE), rows(2, GROUP, TILE_N // LANE), pltpu.VMEM((2, TILE_M, TILE_N), F32),
             dma((4,)), dma((RING,)), dma, dma((2, halves)), dma((RING, halves)), regular,
             dma((2,)), dma((RING,)), regular, dma((7 + ff * LANE // TILE_M,)), dma((4,)), dma((4,)),
-            dma((2, 3)), dma((units,)), dma((stages - 1,)), dma, dma((2,)), dma((2,)), dma((3,)), dma((3,)),
+            dma((2, 3)), dma((units,)), dma((stages - 1,)), dma, dma((2,)), dma((2,)), dma((2,)), dma((2,)),
         ],
         compiler_params=pltpu.CompilerParams(collective_id=0, has_side_effects=True, vmem_limit_bytes=VMEM_BYTES),
         name="pipeline",
@@ -854,7 +855,7 @@
 def finish(lefts, rights, sums, dx):
     units, blocks, height, _ = dx.shape
     halves = height // LANE
-    first_unit = units // GROUP * GROUP
+    first_unit = GROUPS * GROUP
     rest = units - first_unit
     num = len(lefts)
     hbm = pl.BlockSpec(memory_space=pl.ANY)
@@ -865,9 +866,9 @@
         in_specs=[hbm] * (3 * num + 1),
         out_specs=[hbm] * (num + 1),
         scratch_shapes=[
-            pltpu.VMEM((2, rest, halves, TILE_M, LANE), BF16), pltpu.VMEM((2, rest, TILE_N // LANE, height, LANE), BF16),
+            pltpu.VMEM((2, rest, halves, TILE_M, LANE), BF16), pltpu.VMEM((3, rest, TILE_N // LANE, height, LANE), BF16),
             pltpu.VMEM((4, TILE_M, TILE_N), F32), pltpu.VMEM((2, blocks, height, LANE), BF16),
-            dma((2,)), dma((2,)), dma((4,)), dma((4,)), dma((2,)), dma((2,))],
+            dma((2,)), dma((3,)), dma((4,)), dma((4,)), dma((2,)), dma((2,))],
         compiler_params=pltpu.CompilerParams(vmem_limit_bytes=VMEM_BYTES),
         name="finish",
     )(*lefts, *rights, *sums, dx)

time: 634 us -> 631 us (level); the launches traced: 634 us -> 620 us
  Pallas kernels: 632 us -> 618 us
    pallas_call x1, Pallas kernels: 569 us -> 547 us  [run_pipeline(): pl.pallas_call(functools.partial(pipeline_kernel, axis, stages, units, he...]
    pallas_call x1, Pallas kernels: 62.8 us -> 71.6 us  [finish(): pl.pallas_call(functools.partial(finish_kernel, num, first_unit), out_sha...]
where the time goes in v4:
time: 631 us; the launch traced here: 620 us
  Pallas kernels  618 us (98%)
    pallas_call x1, Pallas kernels, run_pipeline(): pl.pallas_call(functools.partial(pipeline_kernel, axis, stages, units, he...  547 us
    pallas_call x1, Pallas kernels, finish(): pl.pallas_call(functools.partial(finish_kernel, num, first_unit), out_sha...  71.6 us

profile of v4, /device:TPU:112, one launch (start us, length us, event | category | flops | bytes accessed | tf_op | source)
XLA Modules:
  0.0 620.5 jit_solution(6391622155999512009)
XLA Ops:
  0.6 546.8 %pipeline.1 = (bf16[16,2,1024,128]{3,2,1,0:T(8,128)(2,1)}, bf16[16,2,1024,128]{3,2,1,0:T(8,128)(2,1)}, bf16[16,2,1024,128]{3,2,1,0:T(8,128)(2,1)}, bf16[16,2,409...) custom-call(bf16[16,256,1024]{2,1,0:T(8,128)(2,1)} %bitcast.12, ...), custom_call_target="tpu_custom_call" | custom-call | tf_op jit(solution)/shard_map/pipeline/pallas_call | solution.py:790
  547.5 1.3 reduce_sum.9
  548.8 71.6 %finish.1 = (f32[1024,3072]{1,0:T(8,128)}, f32[1024,1024]{1,0:T(8,128)}, f32[1024,4096]{1,0:T(8,128)}, f32[4096,1024]{1,0:T(8,128)}, bf16[16,256,1024]{2,1,0:T(8,128)(2,1)}) custom-call(bf16[16,2,1024,128]{3,2,1,0:T(8,128)(2,1)} %get-tuple-element.26.refs_0_, bf16[16,2,1024,128]{3,2,1,0:T(8,128)(2,1)} %get-tuple-element.27.refs_1_, ...), custom_call_target="tpu_custom_call" | custom-call | tf_op jit(solution)/shard_map/finish/pallas_call | solution.py:863
